TPU v7x, 32 devices: a whole 2x2x4 slice. The times are simulated.
32 devices in a mesh: data: 32 (over z, y, x, core).
Axes of the slice: x: 2, y: 2, z: 4, core: 2. Of those that a mesh axis runs over, the one named last changes fastest.
Arguments:
- x_in: bfloat16 [32, 384, 768], P('data')
- grad_y: bfloat16 [32, 384, 768], P('data')
- gain_one: float32 [3, 768], replicated
- gain_two: float32 [3, 768], replicated
- w_qkv: bfloat16 [3, 768, 2304], replicated
- w_out: bfloat16 [3, 768, 768], replicated
- w_up: bfloat16 [3, 768, 3072], replicated
- w_down: bfloat16 [3, 3072, 768], replicated
Outputs:
- output 1: bfloat16 [32, 384, 768], P('data')
- output 2: float32 [3, 768], replicated
- output 3: float32 [3, 768], replicated
- output 4: float32 [3, 768, 2304], replicated
- output 5: float32 [3, 768, 768], replicated
- output 6: float32 [3, 768, 3072], replicated
- output 7: float32 [3, 3072, 768], replicated
All inputs are finite; a program needn't handle non-finite values.
Results may differ from a plain program's by a relative error of at most 0.02.
Values are sent between devices in bfloat16 or wider.
A program may use at most 1 GiB of HBM per device.

v0:
```python
import jax
import jax.numpy as jnp
from jax import lax
from jax.sharding import PartitionSpec as P

NORM_EPS = 1e-6
HEAD_DIM = 64


def rms_gain(rows_f, gain_vec):
    return rows_f * lax.rsqrt(jnp.mean(rows_f * rows_f, axis=-1, keepdims=True) + NORM_EPS) * gain_vec


def gelu_tanh(pre_act):
    return jax.nn.gelu(pre_act, approximate=True)


def mix_lo(einsum_spec, lhs_arr, rhs_arr):
    return jnp.einsum(einsum_spec, lhs_arr, rhs_arr, preferred_element_type=jnp.float32).astype(jnp.bfloat16)


def mix_f32(einsum_spec, lhs_arr, rhs_arr):
    return jnp.einsum(einsum_spec, lhs_arr, rhs_arr, preferred_element_type=jnp.float32)


def block_forward(x_blk, gain_a, gain_b, w_qkv, w_out, w_up):
    n_batch, seq_len, width = x_blk.shape
    head_shape = (n_batch, seq_len, width // HEAD_DIM, HEAD_DIM)
    norm_a, norm_a_back = jax.vjp(rms_gain, x_blk.astype(jnp.float32), gain_a)
    u_one = norm_a.astype(jnp.bfloat16)
    qkv_lo = mix_lo('bsd,de->bse', u_one, w_qkv)
    q_all = qkv_lo[:, :, :width].reshape(head_shape)
    k_all = qkv_lo[:, :, width:2 * width].reshape(head_shape)
    v_all = qkv_lo[:, :, 2 * width:].reshape(head_shape)
    scores = mix_f32('bqhe,bkhe->bhqk', q_all, k_all) * HEAD_DIM ** -0.5
    causal = jnp.arange(seq_len)[:, None] >= jnp.arange(seq_len)[None, :]
    prob_full = jax.nn.softmax(jnp.where(causal, scores, -1e30), axis=-1)
    prob_lo = prob_full.astype(jnp.bfloat16)
    attn_out = mix_lo('bhqk,bkhe->bqhe', prob_lo, v_all).reshape(n_batch, seq_len, width)
    hidden = x_blk + mix_lo('bsd,de->bse', attn_out, w_out)
    norm_b, norm_b_back = jax.vjp(rms_gain, hidden.astype(jnp.float32), gain_b)
    u_two = norm_b.astype(jnp.bfloat16)
    pre_lo = mix_lo('bsd,df->bsf', u_two, w_up)
    act_f, gelu_back = jax.vjp(gelu_tanh, pre_lo.astype(jnp.float32))
    act_lo = act_f.astype(jnp.bfloat16)
    saved_vals = (norm_a_back, u_one, q_all, k_all, v_all, prob_full, prob_lo, attn_out, norm_b_back, u_two, gelu_back, act_lo)
    return hidden, act_lo, saved_vals


def block_backward(grad_blk, saved_vals, w_qkv, w_out, w_up, w_down):
    (norm_a_back, u_one, q_all, k_all, v_all, prob_full, prob_lo, attn_out, norm_b_back, u_two, gelu_back, act_lo) = saved_vals
    n_batch, seq_len, width = grad_blk.shape
    head_shape = (n_batch, seq_len, width // HEAD_DIM, HEAD_DIM)
    grad_down_w = mix_f32('bsf,bsd->fd', act_lo, grad_blk)
    grad_act = mix_lo('bsd,fd->bsf', grad_blk, w_down)
    (grad_pre_f,) = gelu_back(grad_act.astype(jnp.float32))
    grad_pre = grad_pre_f.astype(jnp.bfloat16)
    grad_up_w = mix_f32('bsd,bsf->df', u_two, grad_pre)
    grad_u_two = mix_lo('bsf,df->bsd', grad_pre, w_up)
    grad_h_norm, grad_gain_b = norm_b_back(grad_u_two.astype(jnp.float32))
    grad_hidden = (grad_blk.astype(jnp.float32) + grad_h_norm).astype(jnp.bfloat16)
    grad_out_w = mix_f32('bsd,bse->de', attn_out, grad_hidden)
    grad_attn = mix_lo('bse,de->bsd', grad_hidden, w_out).reshape(head_shape)
    grad_probs = mix_f32('bqhe,bkhe->bhqk', grad_attn, v_all)
    grad_scores = (prob_full * (grad_probs - jnp.sum(prob_full * grad_probs, axis=-1, keepdims=True)) * HEAD_DIM ** -0.5).astype(jnp.bfloat16)
    grad_v = mix_lo('bhqk,bqhe->bkhe', prob_lo, grad_attn)
    grad_q = mix_lo('bhqk,bkhe->bqhe', grad_scores, k_all)
    grad_k = mix_lo('bhqk,bqhe->bkhe', grad_scores, q_all)
    flat_shape = (n_batch, seq_len, width)
    grad_qkv = jnp.concatenate([grad_q.reshape(flat_shape), grad_k.reshape(flat_shape), grad_v.reshape(flat_shape)], axis=-1)
    grad_qkv_w = mix_f32('bsd,bse->de', u_one, grad_qkv)
    grad_u_one = mix_lo('bse,de->bsd', grad_qkv, w_qkv)
    grad_x_norm, grad_gain_a = norm_a_back(grad_u_one.astype(jnp.float32))
    grad_x_blk = (grad_hidden.astype(jnp.float32) + grad_x_norm).astype(jnp.bfloat16)
    return grad_x_blk, (grad_gain_a, grad_gain_b, grad_qkv_w, grad_out_w, grad_up_w, grad_down_w)


def pack_layer(layer_grads):
    return jnp.concatenate([grad_piece.reshape(-1) for grad_piece in reversed(layer_grads)])


def unpack_layer(flat_vals, layer_grads):
    pieces = []
    offset = 0
    for grad_piece in reversed(layer_grads):
        pieces.append(flat_vals[offset:offset + grad_piece.size].reshape(grad_piece.shape))
        offset = offset + grad_piece.size
    return pieces[::-1]


def solution(mesh):
    n_dev = mesh.shape['data']

    def local_step(x_loc, grad_y_loc, gain_one, gain_two, w_qkv, w_out, w_up, w_down):
        n_layers = w_qkv.shape[0]
        hidden_x = x_loc
        saved_all = []
        for layer_idx in range(n_layers):
            hidden, act_lo, saved_vals = block_forward(hidden_x, gain_one[layer_idx], gain_two[layer_idx], w_qkv[layer_idx], w_out[layer_idx], w_up[layer_idx])
            saved_all.append(saved_vals)
            if layer_idx + 1 < n_layers:
                hidden_x = hidden + mix_lo('bsf,fd->bsd', act_lo, w_down[layer_idx])
        grad_cur = grad_y_loc
        reduced_rev = []
        for layer_idx in reversed(range(n_layers)):
            grad_cur, layer_grads = block_backward(grad_cur, saved_all[layer_idx], w_qkv[layer_idx], w_out[layer_idx], w_up[layer_idx], w_down[layer_idx])
            layer_sum = lax.psum(pack_layer(layer_grads), 'data')
            reduced_rev.append(unpack_layer(layer_sum / n_dev, layer_grads))
        reduced = reduced_rev[::-1]
        return (grad_cur,) + tuple(jnp.stack([layer_set[grad_idx] for layer_set in reduced]) for grad_idx in range(6))

    batch_spec = P('data')
    full_spec = P()
    return jax.shard_map(local_step, mesh=mesh, in_specs=(batch_spec, batch_spec) + (full_spec,) * 6, out_specs=(batch_spec,) + (full_spec,) * 6, check_vma=False)
```

profile of v0, /device:TPU:0, one launch (start us, length us, event | category | flops | bytes accessed | tf_op | source)
XLA Modules:
  0.0 1926.3 jit_solution(263700614906880900)
XLA Ops:
  115.1 11.8 fusion.225
  126.9 12.7 fusion.228
  176.4 11.4 fusion.219
  187.8 11.6 fusion.222
  237.8 11.4 fusion.213
  249.2 12.4 fusion.216
  320.5 7.9 reshape.809
  328.5 7.9 reshape.805
  336.4 9.6 copy.87
  346.0 9.6 copy.88
  361.6 10.8 reshape.802
  372.3 10.8 reshape.806
  383.1 10.7 reshape.810
  393.8 8.3 constant_dynamic-update-slice_fusion.17
  407.4 8.4 constant_dynamic-update-slice_fusion.15
  447.8 10.3 constant_dynamic-update-slice_fusion.6
  463.3 1193.3 %all-reduce.3.cloned.1.call-done = (f32[7079424]{0:T(1024)}, f32[7079424]{0:T(1024)}, f32[7079424]{0:T(1024)}) async-done(((f32[7079424]{0:T(1024)}, f32[7079424]{0:T(1024)}, f32[7079424]{0:T(1024)}), (f32[7079424]{0:T(1024)}, f32[7079424]{0:T(1024)}, f32[7079424]{0:T(1024)})) %all-reduce.3.cloned.1.call-update) | async-done | bytes 84953104 | tf_op jit(solution)/shard_map/psum | solution.py:107
  1656.6 38.6 %broadcast_multiply_fusion = (f32[7079424]{0:T(1024)}, f32[7079424]{0:T(1024)}) fusion(f32[7079424]{0:T(1024)} %get-tuple-element.25, f32[7079424]{0:T(1024)} %get-tuple-element.26), kind=kLoop, calls=%fused_computation.9 | loop fusion | flops 14158848 | bytes 113270784 | tf_op jit(solution)/shard_map/div | solution.py:108
  1709.3 15.8 fusion.411
  1739.3 10.4 broadcast_multiply_fusion.2
  1767.3 11.3 stack_reshape.47
  1778.5 8.2 stack_reshape.38
  1786.8 11.3 stack_reshape.46
  1798.1 8.2 stack_reshape.37
  1806.3 10.9 stack_reshape.43
  1817.2 10.9 stack_reshape.44
  1831.5 11.3 stack_reshape.45
  1842.8 8.2 stack_reshape.36
  1851.0 10.9 stack_reshape.42
  1869.2 23.8 %pad_maximum_fusion.1 = f32[3,3072,768]{2,1,0:T(8,128)} fusion(f32[1,3072,768]{2,1,0:T(8,128)} %stack_reshape.47, f32[1,3072,768]{2,1,0:T(8,128)} %stack_reshape.46, f32[1,3072,768]{2,1,0:T(8,128)} %stack_reshape.45), kind=kLoop, calls=%fused_computation.7 | loop fusion | flops 14155776 | bytes 56623104 | tf_op jit(solution)/shard_map/stack | solution.py:110
  1893.0 16.4 pad_maximum_fusion.2
  1909.4 9.8 pad_maximum_fusion
  (387 shorter events, 345.4 us)
Async XLA Ops:
  7.2 1649.5 %all-reduce.3.cloned.1.call-start = ((), (), s32[]{:S(2)}) async-start(), calls=%async_computation | async-start | bytes 169918464 | tf_op jit(solution)/shard_map/psum | solution.py:107
  10.3 15.7 copy-start.48
  10.4 89.8 %copy-start.46 = (f32[768]{0:T(1024)}, f32[768]{0:T(1024)S(1)}, u32[]{:S(2)}) copy-start(f32[768]{0:T(1024)S(1)} %get-tuple-element.19) | copy-start | bytes 9220
  82.2 18.0 copy-start.13
  82.2 18.0 copy-start.58
  126.9 12.7 copy-start.25
  126.9 12.7 copy-start.23
  126.9 12.7 copy-start.67
  144.8 12.9 copy-start.21
  336.4 19.2 slice-start.19
  336.4 19.2 slice-start.20
  402.1 13.8 slice-start.22
  402.1 13.8 slice-start.23
  440.5 17.8 copy-start
  1703.3 21.8 %slice-start = ((s8[28319744]{0:T(1024)(128)(4,1)}), s8[4194304]{0:T(1024)(128)(4,1)S(1)}, s32[]{:S(2)}) async-start(s8[28319744]{0:T(1024)(128)(4,1)} %bitcast.451), calls=%async_computation.1 | async-start | bytes 8388608
  1703.3 21.8 %slice-start.1 = ((s8[28319744]{0:T(1024)(128)(4,1)}), s8[4194304]{0:T(1024)(128)(4,1)S(1)}, s32[]{:S(2)}) async-start(s8[28319744]{0:T(1024)(128)(4,1)} %bitcast.451), calls=%async_computation.2 | async-start | bytes 8388608
  1709.2 15.8 slice-start.2
  1709.2 16.0 slice-start.3
  1709.2 17.9 slice-start.4
  1709.3 19.1 slice-start.5
  1709.3 20.0 %slice-start.6 = ((s8[28319744]{0:T(1024)(128)(4,1)}), s8[3153920]{0:T(1024)(128)(4,1)S(1)}, s32[]{:S(2)}) async-start(s8[28319744]{0:T(1024)(128)(4,1)} %bitcast.451), calls=%async_computation.7 | async-start | bytes 6307840
  1863.2 29.8 %slice-start.25 = ((s8[7077888]{0:T(1024)(128)(4,1)}), s8[4194304]{0:T(1024)(128)(4,1)S(1)}, s32[]{:S(2)}) async-start(s8[7077888]{0:T(1024)(128)(4,1)} %bitcast.468), calls=%async_computation.26 | async-start | bytes 8388608
  1869.1 23.8 %slice-start.26 = ((s8[7077888]{0:T(1024)(128)(4,1)}), s8[2883584]{0:T(1024)(128)(4,1)S(1)}, s32[]{:S(2)}) async-start(s8[7077888]{0:T(1024)(128)(4,1)} %bitcast.468), calls=%async_computation.27 | async-start | bytes 5767168
  1869.1 40.2 %slice-start.7 = ((s8[9437184]{0:T(1024)(128)(4,1)}), s8[4194304]{0:T(1024)(128)(4,1)S(1)}, s32[]{:S(2)}) async-start(s8[9437184]{0:T(1024)(128)(4,1)} %bitcast.453), calls=%async_computation.8 | async-start | bytes 8388608
  1869.1 40.2 %slice-start.8 = ((s8[9437184]{0:T(1024)(128)(4,1)}), s8[4194304]{0:T(1024)(128)(4,1)S(1)}, s32[]{:S(2)}) async-start(s8[9437184]{0:T(1024)(128)(4,1)} %bitcast.453), calls=%async_computation.9 | async-start | bytes 8388608
  1869.1 40.2 %slice-start.10 = ((s8[9437184]{0:T(1024)(128)(4,1)}), s8[4194304]{0:T(1024)(128)(4,1)S(1)}, s32[]{:S(2)}) async-start(s8[9437184]{0:T(1024)(128)(4,1)} %bitcast.455), calls=%async_computation.11 | async-start | bytes 8388608
  1869.1 40.2 %slice-start.11 = ((s8[9437184]{0:T(1024)(128)(4,1)}), s8[4194304]{0:T(1024)(128)(4,1)S(1)}, s32[]{:S(2)}) async-start(s8[9437184]{0:T(1024)(128)(4,1)} %bitcast.455), calls=%async_computation.12 | async-start | bytes 8388608
  1869.2 40.2 %slice-start.13 = ((s8[9437184]{0:T(1024)(128)(4,1)}), s8[4194304]{0:T(1024)(128)(4,1)S(1)}, s32[]{:S(2)}) async-start(s8[9437184]{0:T(1024)(128)(4,1)} %bitcast.457), calls=%async_computation.14 | async-start | bytes 8388608
  1869.2 40.2 %slice-start.14 = ((s8[9437184]{0:T(1024)(128)(4,1)}), s8[4194304]{0:T(1024)(128)(4,1)S(1)}, s32[]{:S(2)}) async-start(s8[9437184]{0:T(1024)(128)(4,1)} %bitcast.457), calls=%async_computation.15 | async-start | bytes 8388608
  1892.9 16.4 slice-start.9
  1893.0 16.4 slice-start.12
  1893.0 16.4 slice-start.15
  (94 other events, 501.8 us)
Sparse Core Ops, SparseCore 0:
  461.0 1195.5 all-reduce.2
where the time goes:
time: 1930 us
  waiting for transfers between devices  1190 us (62%)
  local copies, waits for them, and re-layouts  323 us (17%)
  matrix products  283 us (15%)
  other arithmetic  111 us (6%)
    psum x1, waiting for transfers between devices, local_step(): layer_sum = lax.psum(pack_layer(layer_grads), 'data')  1190 us
    dot_general x35, matrix products, mix_lo(): jnp.einsum(einsum_spec, lhs_arr, rhs_arr, preferred_element_type=jnp.floa...  200 us
    another operation x18, local copies, waits for them, and re-layouts, local_step(): jnp.stack([layer_set[grad_idx] for layer_set in reduced])  101 us
    unnamed x268, local copies, waits for them, and re-layouts  96.6 us
    dot_general x15, matrix products, mix_f32(): jnp.einsum(einsum_spec, lhs_arr, rhs_arr, preferred_element_type=jnp.floa...  67 us
    reshape x9, local copies, waits for them, and re-layouts, pack_layer(): grad_piece.reshape(-1)  63.1 us
    another operation x6, other arithmetic, local_step(): jnp.stack([layer_set[grad_idx] for layer_set in reduced])  57.1 us
    slice x12, local copies, waits for them, and re-layouts, unpack_layer(): flat_vals[offset:offset + grad_piece.size].reshape(grad_piece.shape)  51.5 us
  transfers between devices with their start and end apart: 1, of which 1 were waited for; matrix products, arithmetic and copies ran while one was open for 0% of the time, Pallas kernels for 0%

commit v1 on v0

--- a/solution.py
+++ b/solution.py
@@ -1,10 +1,20 @@
+import functools
+
 import jax
 import jax.numpy as jnp
 from jax import lax
+from jax.experimental import pallas as pl
+from jax.experimental.pallas import tpu as pltpu
 from jax.sharding import PartitionSpec as P
 
 NORM_EPS = 1e-6
 HEAD_DIM = 64
+WIDTH = 768
+TILES = 12
+SUB = 16
+RING = 16
+HOP = 2
+MESH_ID = pl.DeviceIdType.MESH
 
 
 def rms_gain(rows_f, gain_vec):
@@ -51,15 +61,12 @@
     (norm_a_back, u_one, q_all, k_all, v_all, prob_full, prob_lo, attn_out, norm_b_back, u_two, gelu_back, act_lo) = saved_vals
     n_batch, seq_len, width = grad_blk.shape
     head_shape = (n_batch, seq_len, width // HEAD_DIM, HEAD_DIM)
-    grad_down_w = mix_f32('bsf,bsd->fd', act_lo, grad_blk)
     grad_act = mix_lo('bsd,fd->bsf', grad_blk, w_down)
     (grad_pre_f,) = gelu_back(grad_act.astype(jnp.float32))
     grad_pre = grad_pre_f.astype(jnp.bfloat16)
-    grad_up_w = mix_f32('bsd,bsf->df', u_two, grad_pre)
     grad_u_two = mix_lo('bsf,df->bsd', grad_pre, w_up)
     grad_h_norm, grad_gain_b = norm_b_back(grad_u_two.astype(jnp.float32))
     grad_hidden = (grad_blk.astype(jnp.float32) + grad_h_norm).astype(jnp.bfloat16)
-    grad_out_w = mix_f32('bsd,bse->de', attn_out, grad_hidden)
     grad_attn = mix_lo('bse,de->bsd', grad_hidden, w_out).reshape(head_shape)
     grad_probs = mix_f32('bqhe,bkhe->bhqk', grad_attn, v_all)
     grad_scores = (prob_full * (grad_probs - jnp.sum(prob_full * grad_probs, axis=-1, keepdims=True)) * HEAD_DIM ** -0.5).astype(jnp.bfloat16)
@@ -68,24 +75,352 @@
     grad_k = mix_lo('bhqk,bqhe->bkhe', grad_scores, q_all)
     flat_shape = (n_batch, seq_len, width)
     grad_qkv = jnp.concatenate([grad_q.reshape(flat_shape), grad_k.reshape(flat_shape), grad_v.reshape(flat_shape)], axis=-1)
-    grad_qkv_w = mix_f32('bsd,bse->de', u_one, grad_qkv)
     grad_u_one = mix_lo('bse,de->bsd', grad_qkv, w_qkv)
     grad_x_norm, grad_gain_a = norm_a_back(grad_u_one.astype(jnp.float32))
     grad_x_blk = (grad_hidden.astype(jnp.float32) + grad_x_norm).astype(jnp.bfloat16)
-    return grad_x_blk, (grad_gain_a, grad_gain_b, grad_qkv_w, grad_out_w, grad_up_w, grad_down_w)
-
-
-def pack_layer(layer_grads):
-    return jnp.concatenate([grad_piece.reshape(-1) for grad_piece in reversed(layer_grads)])
-
-
-def unpack_layer(flat_vals, layer_grads):
-    pieces = []
-    offset = 0
-    for grad_piece in reversed(layer_grads):
-        pieces.append(flat_vals[offset:offset + grad_piece.size].reshape(grad_piece.shape))
-        offset = offset + grad_piece.size
-    return pieces[::-1]
+    factors = (u_one, grad_qkv, attn_out, grad_hidden, u_two, grad_pre, act_lo, grad_blk)
+    return grad_x_blk, grad_gain_a, grad_gain_b, factors
+
+
+def layer_tiles(factors):
+    u_one, grad_qkv, attn_out, grad_hidden, u_two, grad_pre, act_lo, grad_blk = factors
+    tiles = []
+    for lhs, rhs in ((u_one, grad_qkv), (attn_out, grad_hidden), (u_two, grad_pre), (act_lo, grad_blk)):
+        tiles += [(lhs, left, rhs, right) for left in range(0, lhs.shape[1], WIDTH) for right in range(0, rhs.shape[1], WIDTH)]
+    return tiles
+
+
+def reduce_kernel(n_tile, n_dev, *refs):
+    n_factor = 8 * (-(-n_tile // TILES))
+    reduce_body(n_tile, n_dev, refs[:n_factor], *refs[n_factor:])
+
+
+def reduce_body(n_tile, n_dev, f_refs, g_ref, fa, fb, part, ra, acc, rzb, rza, rb, fin,
+                  fl_a, fl_b, fs_a, fs_b, fr_a, fr_b,
+                  ra_s, ra_r, z_s, zb_r, za_r, b_s, b_r, bag_s, bag_r, loc, bc_r, up_s, dn_s, aag_s, aag_r, p1_s, p1_r, p2_s, p2_r):
+    toks = f_refs[0].shape[0]
+    half = WIDTH // 2
+    n_slot = fa.shape[0]
+    tiles = [tile for lo in range(0, len(f_refs), 8) for tile in layer_tiles(f_refs[lo:lo + 8])][:n_tile]
+    per_tile = half // (8 * SUB)
+    n_unit = n_tile * per_tile
+    me = lax.axis_index('data')
+    core, my_x, my_y, my_z = me % 2, (me // 2) % 2, (me // 4) % 2, me // 8
+    top_z = n_dev // 8 - 1
+    x_dev, y_dev, pair_dev = me + 2 - 4 * my_x, me + 4 - 8 * my_y, me + 1 - 2 * core
+    up_dev, dn_dev = me + 8, me - 8
+
+    barrier = pltpu.get_barrier_semaphore()
+    for dev in (x_dev, y_dev, pair_dev):
+        pl.semaphore_signal(barrier, inc=1, device_id=(dev,), device_id_type=MESH_ID)
+
+    @pl.when(my_z < top_z)
+    def _():
+        pl.semaphore_signal(barrier, inc=1, device_id=(up_dev,), device_id_type=MESH_ID)
+
+    @pl.when(my_z > 0)
+    def _():
+        pl.semaphore_signal(barrier, inc=1, device_id=(dn_dev,), device_id_type=MESH_ID)
+
+    pl.semaphore_wait(barrier, 3 + jnp.where(my_z < top_z, 1, 0) + jnp.where(my_z > 0, 1, 0))
+
+    def remote(src, dst, send_sem, recv_sem, dev):
+        return pltpu.make_async_remote_copy(src_ref=src, dst_ref=dst, send_sem=send_sem, recv_sem=recv_sem, device_id=(dev,), device_id_type=MESH_ID)
+
+    def factor_copies(slot, source):
+        lhs, left, rhs, right = source
+        mine = pl.ds(pl.multiple_of(left + core * half, 128), half)
+        other = pl.ds(pl.multiple_of(left + (1 - core) * half, 128), half)
+        lo, hi = pl.ds(0, toks), pl.ds(toks, toks)
+        cols = pl.ds(right, WIDTH)
+        return (
+            pltpu.make_async_copy(lhs.at[:, mine], fa.at[slot, lo], fl_a.at[slot]),
+            pltpu.make_async_copy(rhs.at[:, cols], fb.at[slot, lo], fl_b.at[slot]),
+            remote(lhs.at[:, other], fa.at[slot, hi], fs_a.at[slot], fr_a.at[slot], pair_dev),
+            remote(rhs.at[:, cols], fb.at[slot, hi], fs_b.at[slot], fr_b.at[slot], pair_dev),
+        )
+
+    for tile in range(2):
+        for copy in factor_copies(tile, tiles[tile]):
+            copy.start()
+
+    def stream_stages(s):
+        my_a, my_b = (my_x, my_y) if s == 0 else (my_y, my_x)
+        a_dev, b_dev = (x_dev, y_dev) if s == 0 else (y_dev, x_dev)
+
+        def root_of(u):
+            return (u + 2 * s) % (top_z + 1)
+
+        def part_rows(u, side):
+            return pl.ds(pl.multiple_of((u % per_tile) * (8 * SUB) + s * (4 * SUB) + side * (2 * SUB), 8), 2 * SUB)
+
+        def part_at(u, side):
+            return part.at[(u // per_tile) % 2, part_rows(u, side)]
+
+        def out_at(u, which, side, b_side=None):
+            base = (u // per_tile) * WIDTH + which * half + (u % per_tile) * (8 * SUB) + s * (4 * SUB) + side * (2 * SUB)
+            if b_side is None:
+                return g_ref.at[pl.ds(pl.multiple_of(base, 8), 2 * SUB)]
+            return g_ref.at[pl.ds(pl.multiple_of(base + b_side * SUB, 8), SUB)]
+
+        def a_copy(u):
+            k = u % RING
+            return remote(part_at(u, 1 - my_a), ra.at[s, k], ra_s.at[s, k], ra_r.at[s, k], a_dev)
+
+        def up_copy(u):
+            k = u % RING
+            return remote(acc.at[s, k], rzb.at[s, k], z_s.at[s, k], zb_r.at[s, k], up_dev)
+
+        def dn_copy(u):
+            k = u % RING
+            return remote(acc.at[s, k], rza.at[s, k], z_s.at[s, k], za_r.at[s, k], dn_dev)
+
+        def b_rows(side):
+            return pl.ds(pl.multiple_of(side * SUB, 8), SUB)
+
+        def b_copy(u):
+            k = u % RING
+            return remote(acc.at[s, k, b_rows(1 - my_b)], rb.at[s, k], b_s.at[s, k], b_r.at[s, k], b_dev)
+
+        def bag_copy(u, b_side):
+            k = u % RING
+            return remote(fin.at[s, k], out_at(u, core, my_a, b_side), bag_s.at[s, k], bag_r.at[s, k], b_dev)
+
+        def loc_copy(u):
+            k = u % RING
+            return pltpu.make_async_copy(fin.at[s, k], out_at(u, core, my_a, my_b), loc.at[s, k])
+
+        def cast_up(u):
+            k = u % RING
+            rows = out_at(u, core, my_a)
+            return remote(rows, rows, up_s.at[s, k], bc_r.at[s, k], up_dev)
+
+        def cast_dn(u):
+            k = u % RING
+            rows = out_at(u, core, my_a)
+            return remote(rows, rows, dn_s.at[s, k], bc_r.at[s, k], dn_dev)
+
+        def aag_copy(u, side):
+            k = u % RING
+            rows = out_at(u, core, side)
+            return remote(rows, rows, aag_s.at[s, k], aag_r.at[s, k], a_dev)
+
+        def p1_copy(u, which):
+            k = u % RING
+            rows = out_at(u, which, my_a)
+            return remote(rows, rows, p1_s.at[s, k], p1_r.at[s, k], pair_dev)
+
+        def p2_copy(u, which):
+            k = u % RING
+            rows = out_at(u, which, 1 - my_a)
+            return remote(rows, rows, p2_s.at[s, k], p2_r.at[s, k], pair_dev)
+
+        def z_send(u, root):
+            @pl.when(my_z < root)
+            def _():
+                up_copy(u).start()
+
+            @pl.when(my_z > root)
+            def _():
+                dn_copy(u).start()
+
+        def take_below(u):
+            k = u % RING
+            up_copy(u).wait_recv()
+            acc[s, k] = acc[s, k] + rzb[s, k]
+
+        def take_above(u):
+            k = u % RING
+            dn_copy(u).wait_recv()
+            acc[s, k] = acc[s, k] + rza[s, k]
+
+        def stage_first(u):
+            a_copy(u).start()
+
+        def stage_pair(u):
+            k = u % RING
+            root = root_of(u)
+            a_copy(u).wait_recv()
+            acc[s, k] = part[(u // per_tile) % 2, part_rows(u, my_a)] + ra[s, k]
+            a_copy(u).wait_send()
+
+            @pl.when((my_z == 0) | (my_z == top_z))
+            def _():
+                z_send(u, root)
+
+        def stage_line(level, u):
+            root = root_of(u)
+
+            @pl.when((my_z < root) & (my_z == level))
+            def _():
+                take_below(u)
+                up_copy(u).start()
+
+            @pl.when((my_z > root) & (top_z - my_z == level))
+            def _():
+                take_above(u)
+                dn_copy(u).start()
+
+        def stage_root(u):
+            @pl.when(my_z == root_of(u))
+            def _():
+                @pl.when(my_z > 0)
+                def _():
+                    take_below(u)
+
+                @pl.when(my_z < top_z)
+                def _():
+                    take_above(u)
+
+                b_copy(u).start()
+
+        def stage_final(u):
+            k = u % RING
+
+            @pl.when(my_z == root_of(u))
+            def _():
+                b_copy(u).wait_recv()
+                fin[s, k] = (acc[s, k, b_rows(my_b)] + rb[s, k]) * (1.0 / n_dev)
+                bag_copy(u, my_b).start()
+                loc_copy(u).start()
+                b_copy(u).wait_send()
+
+        def send_on(u, root):
+            @pl.when((my_z >= root) & (my_z < top_z))
+            def _():
+                cast_up(u).start()
+
+            @pl.when((my_z <= root) & (my_z > 0))
+            def _():
+                cast_dn(u).start()
+
+            aag_copy(u, my_a).start()
+            p1_copy(u, core).start()
+
+        def stage_cast(dist, u):
+            root = root_of(u)
+            if dist == 0:
+                @pl.when(my_z == root)
+                def _():
+                    loc_copy(u).wait()
+                    bag_copy(u, my_b).wait_send()
+                    bag_copy(u, 1 - my_b).wait_recv()
+                    send_on(u, root)
+            else:
+                @pl.when((my_z == root + dist) | (my_z == root - dist))
+                def _():
+                    cast_up(u).wait_recv()
+                    up_copy(u).wait_send()
+                    send_on(u, root)
+
+        def stage_swap(u):
+            aag_copy(u, 1 - my_a).wait_recv()
+            p2_copy(u, core).start()
+
+        def stage_done(u):
+            root = root_of(u)
+            p1_copy(u, 1 - core).wait_recv()
+            p2_copy(u, 1 - core).wait_recv()
+
+            @pl.when((my_z >= root) & (my_z < top_z))
+            def _():
+                cast_up(u).wait_send()
+
+            @pl.when((my_z <= root) & (my_z > 0))
+            def _():
+                cast_dn(u).wait_send()
+
+            aag_copy(u, my_a).wait_send()
+            p1_copy(u, core).wait_send()
+            p2_copy(u, core).wait_send()
+
+        stages = [stage_first, stage_pair]
+        stages += [functools.partial(stage_line, level) for level in range(1, top_z)]
+        stages += [stage_root, stage_final]
+        stages += [functools.partial(stage_cast, dist) for dist in range(top_z + 1)]
+        stages += [stage_swap, stage_done]
+        return stages
+
+    streams = [stream_stages(0), stream_stages(1)]
+    n_stage = len(streams[0])
+
+    def step(t, carry):
+        tile = t // per_tile
+
+        for stage_idx in reversed(range(1, n_stage)):
+            u = t - HOP * stage_idx
+
+            @pl.when((u >= 0) & (u < n_unit))
+            def _():
+                for stages in streams:
+                    stages[stage_idx](u)
+
+        @pl.when((t < n_unit) & (t % per_tile == 0))
+        def _():
+            slot = tile % n_slot
+            for copy in factor_copies(slot, tiles[0]):
+                copy.wait()
+            for lo in range(0, half, 128):
+                part[tile % 2, lo:lo + 128, :] = lax.dot_general(
+                    fa[slot, :, lo:lo + 128], fb[slot], (((0,), (0,)), ((), ())), preferred_element_type=jnp.float32)
+
+            for later in range(2, n_tile):
+                @pl.when(tile + 2 == later)
+                def _():
+                    for copy in factor_copies(later % n_slot, tiles[later]):
+                        copy.start()
+
+        @pl.when(t < n_unit)
+        def _():
+            for stages in streams:
+                stages[0](t)
+
+        return carry
+
+    lax.fori_loop(0, n_unit + HOP * (n_stage - 1), step, 0)
+
+
+def reduce_tiles(factors, n_tile, n_dev):
+    toks = factors[0].shape[0]
+    half = WIDTH // 2
+    f32, bf16 = jnp.float32, jnp.bfloat16
+    dma = pltpu.SemaphoreType.DMA
+    slots = pltpu.VMEM((2, RING, 2 * SUB, WIDTH), f32)
+    flops = n_tile * 2 * half * 2 * toks * WIDTH
+    return pl.pallas_call(
+        functools.partial(reduce_kernel, n_tile, n_dev),
+        out_shape=jax.ShapeDtypeStruct((n_tile * WIDTH, WIDTH), f32),
+        in_specs=[pl.BlockSpec(memory_space=pl.ANY)] * len(factors),
+        out_specs=pl.BlockSpec(memory_space=pl.ANY),
+        scratch_shapes=[
+            pltpu.VMEM((4, 2 * toks, half), bf16),
+            pltpu.VMEM((4, 2 * toks, WIDTH), bf16),
+            pltpu.VMEM((2, half, WIDTH), f32),
+            slots, slots, slots, slots,
+            pltpu.VMEM((2, RING, SUB, WIDTH), f32),
+            pltpu.VMEM((2, RING, SUB, WIDTH), f32),
+        ] + [dma((4,))] * 6 + [dma((2, RING))] * 19,
+        compiler_params=pltpu.CompilerParams(collective_id=0, has_side_effects=True, vmem_limit_bytes=48 * 1024 * 1024),
+        cost_estimate=pl.CostEstimate(flops=flops, bytes_accessed=n_tile * WIDTH * WIDTH * 8, transcendentals=0),
+        name='reduce_tiles',
+    )(*factors)
+
+
+def copy_block(src_ref, dst_ref):
+    dst_ref[0] = src_ref[0, 0]
+
+
+def spread_tiles(tiles, first, count, down=False):
+    n_layers = tiles.shape[0]
+    shape = (n_layers, count * WIDTH, WIDTH) if down else (n_layers, WIDTH, count * WIDTH)
+    return pl.pallas_call(
+        copy_block,
+        grid=(n_layers, count),
+        out_shape=jax.ShapeDtypeStruct(shape, tiles.dtype),
+        in_specs=[pl.BlockSpec((1, 1, WIDTH, WIDTH), lambda layer, j: (layer, first + j, 0, 0))],
+        out_specs=pl.BlockSpec((1, WIDTH, WIDTH), (lambda layer, j: (layer, j, 0)) if down else (lambda layer, j: (layer, 0, j))),
+        name='spread_tiles',
+    )(tiles)
 
 
 def solution(mesh):
@@ -101,13 +436,16 @@
             if layer_idx + 1 < n_layers:
                 hidden_x = hidden + mix_lo('bsf,fd->bsd', act_lo, w_down[layer_idx])
         grad_cur = grad_y_loc
-        reduced_rev = []
+        all_factors = [None] * n_layers
+        gain_grads = [None] * (2 * n_layers)
         for layer_idx in reversed(range(n_layers)):
-            grad_cur, layer_grads = block_backward(grad_cur, saved_all[layer_idx], w_qkv[layer_idx], w_out[layer_idx], w_up[layer_idx], w_down[layer_idx])
-            layer_sum = lax.psum(pack_layer(layer_grads), 'data')
-            reduced_rev.append(unpack_layer(layer_sum / n_dev, layer_grads))
-        reduced = reduced_rev[::-1]
-        return (grad_cur,) + tuple(jnp.stack([layer_set[grad_idx] for layer_set in reduced]) for grad_idx in range(6))
+            grad_cur, gain_grads[layer_idx], gain_grads[n_layers + layer_idx], factors = block_backward(grad_cur, saved_all[layer_idx], w_qkv[layer_idx], w_out[layer_idx], w_up[layer_idx], w_down[layer_idx])
+            all_factors[layer_idx] = [factor.reshape(factor.shape[1:]) for factor in factors]
+        gain_sum = lax.psum(jnp.stack(gain_grads), 'data') / n_dev
+        tiles = reduce_tiles([factor for layer in all_factors for factor in layer], n_layers * TILES, n_dev).reshape(n_layers, TILES, WIDTH, WIDTH)
+
+        return (grad_cur, gain_sum[:n_layers], gain_sum[n_layers:], spread_tiles(tiles, 0, 3), spread_tiles(tiles, 3, 1), spread_tiles(tiles, 4, 4),
+                spread_tiles(tiles, 8, 4, down=True))
 
     batch_spec = P('data')
     full_spec = P()

time: 1930 us -> 958 us (0.50)
  waiting for transfers between devices: 1190 us -> 0 us
  Pallas kernels: 0 us -> 620 us
  local copies, waits for them, and re-layouts: 323 us -> 38.6 us
  other arithmetic: 111 us -> 11.3 us
  matrix products: 283 us -> 238 us
  blocking collectives: 0 us -> 42.8 us
    psum x1 -> x0, waiting for transfers between devices: 1190 us -> none  [local_step(): layer_sum = lax.psum(pack_layer(layer_grads), 'data')]
    pallas_call x0 -> x5, Pallas kernels: none -> 620 us  [the longest x1 551 us: reduce_tiles(): pl.pallas_call(functools.partial(reduce_kernel, n_tile, n_dev), out_shape...]
    another operation x18 -> x10, local copies, waits for them, and re-layouts: 101 us -> 7.3 us  [the longest x7 4.85 us: local_step(): gain_sum = lax.psum(jnp.stack(gain_grads), 'data') / n_dev]
    unnamed x268 -> x156, local copies, waits for them, and re-layouts: 96.6 us -> 4.99 us
    dot_general x15 -> x3, matrix products: 67 us -> 14.4 us  [mix_f32(): jnp.einsum(einsum_spec, lhs_arr, rhs_arr, preferred_element_type=jnp.floa...]
    another operation x6 -> x8, other arithmetic: 57.1 us -> 5.84 us  [local_step(): jnp.stack([layer_set[grad_idx] for layer_set in reduced])]
    slice x12 -> x1, local copies, waits for them, and re-layouts: 51.5 us -> 0.61 us  [local_step(): gain_sum[n_layers:]]
    div x2 -> x1, other arithmetic: 49 us -> 0.74 us  [local_step(): gain_sum = lax.psum(jnp.stack(gain_grads), 'data') / n_dev]
  transfers between devices with their start and end apart: 1 -> 0, of which waited for: 1 -> 0; matrix products, arithmetic and copies ran while one was open for 0% -> 0% of each run, Pallas kernels for 0% -> 0%
where the time goes in v1:
time: 958 us; the launch traced here: 953 us
  Pallas kernels  620 us (65%)
  matrix products  238 us (25%)
  blocking collectives  42.8 us (4%)
  local copies, waits for them, and re-layouts  38.6 us (4%)
  other arithmetic  11.3 us (1%)
    pallas_call x1, Pallas kernels, reduce_tiles(): pl.pallas_call(functools.partial(reduce_kernel, n_tile, n_dev), out_shape...  551 us
    dot_general x35, matrix products, mix_lo(): jnp.einsum(einsum_spec, lhs_arr, rhs_arr, preferred_element_type=jnp.floa...  206 us
    pallas_call x4, Pallas kernels, spread_tiles(): pl.pallas_call(copy_block, grid=(n_layers, count), out_shape=jax.ShapeDty...  69.2 us
    psum x1, blocking collectives, local_step(): gain_sum = lax.psum(jnp.stack(gain_grads), 'data') / n_dev  42.8 us

profile of v1, /device:TPU:0, one launch (start us, length us, event | category | flops | bytes accessed | tf_op | source)
XLA Modules:
  0.0 952.9 jit_solution(8812903732676403020)
XLA Ops:
  9.9 5.0 fusion.369
  21.3 7.0 fusion.30
  28.3 6.3 fusion.301
  39.7 5.5 fusion.370
  52.3 7.0 fusion.36
  59.4 6.3 fusion.305
  71.9 7.0 fusion.371
  86.1 7.0 fusion.44
  93.0 6.5 fusion.17.refs_21_
  99.6 5.4 fusion.268
  108.5 5.2 fusion.204
  119.2 12.4 %fusion.219 = bf16[12,64,384]{2,1,0:T(8,128)(2,1)} fusion(bf16[384,12,64]{0,2,1:T(8,128)(2,1)} %bitcast.449, f32[12,384,384]{1,2,0:T(8,128)} %fusion.372, f32[12,384,384]{1,2,0:T(8,128)} %get-tuple-element.49, f32[12,384]{1,0:T(8,128)} %get-tuple-element.48), kind=kOutput, calls=%fused_computation.244 | convolution fusion | flops 239178624 | bytes 15353856 | tf_op jit(solution)/shard_map/bhqk,bkhe->bqhe/dot_general | solution.py:29
  131.6 12.3 %fusion.222 = bf16[12,64,384]{2,1,0:T(8,128)(2,1)} fusion(bf16[384,12,64]{0,2,1:T(8,128)(2,1)S(1)} %bitcast.451, f32[12,384,384]{1,2,0:T(8,128)} %fusion.372, f32[12,384,384]{1,2,0:T(8,128)} %get-tuple-element.49, f32[12,384]{1,0:T(8,128)S(1)} %copy-done.77), kind=kOutput, calls=%fused_computation.245 | convolution fusion | flops 239178624 | bytes 15353856 | tf_op jit(solution)/shard_map/bhqk,bqhe->bkhe/dot_general | solution.py:29
  151.7 6.3 fusion.20.refs_13_
  158.1 5.4 fusion.272
  169.4 5.3 fusion.198
  176.8 5.2 fusion.373
  182.0 12.3 %fusion.213 = bf16[12,64,384]{2,1,0:T(8,128)(2,1)} fusion(bf16[384,12,64]{0,2,1:T(8,128)(2,1)} %bitcast.445, f32[12,384,384]{1,2,0:T(8,128)} %fusion.373, f32[12,384,384]{1,2,0:T(8,128)} %get-tuple-element.43, f32[12,384]{1,0:T(8,128)} %copy-done.76), kind=kOutput, calls=%fused_computation.242 | convolution fusion | flops 239178624 | bytes 15353856 | tf_op jit(solution)/shard_map/bhqk,bkhe->bqhe/dot_general | solution.py:29
  194.2 12.3 %fusion.216 = bf16[12,64,384]{2,1,0:T(8,128)(2,1)} fusion(bf16[384,12,64]{0,2,1:T(8,128)(2,1)} %bitcast.447, f32[12,384,384]{1,2,0:T(8,128)} %fusion.373, f32[12,384,384]{1,2,0:T(8,128)} %get-tuple-element.43, f32[12,384]{1,0:T(8,128)} %copy-done.76), kind=kOutput, calls=%fused_computation.243 | convolution fusion | flops 239178624 | bytes 15353856 | tf_op jit(solution)/shard_map/bhqk,bqhe->bkhe/dot_general | solution.py:29
  216.3 6.3 fusion.23.refs_5_
  224.9 4.6 fusion.276
  233.5 5.3 fusion.192
  240.9 5.2 fusion.374
  246.1 12.4 %fusion.207 = bf16[12,64,384]{2,1,0:T(8,128)(2,1)} fusion(bf16[384,12,64]{0,2,1:T(8,128)(2,1)} %bitcast.441, f32[12,384,384]{1,2,0:T(8,128)} %fusion.374, f32[12,384,384]{1,2,0:T(8,128)} %get-tuple-element.37, f32[12,384]{1,0:T(8,128)} %copy-done.75), kind=kOutput, calls=%fused_computation.240 | convolution fusion | flops 239178624 | bytes 15353856 | tf_op jit(solution)/shard_map/bhqk,bkhe->bqhe/dot_general | solution.py:29
  258.5 12.4 %fusion.210 = bf16[12,64,384]{2,1,0:T(8,128)(2,1)} fusion(bf16[384,12,64]{0,2,1:T(8,128)(2,1)} %bitcast.443, f32[12,384,384]{1,2,0:T(8,128)} %fusion.374, f32[12,384,384]{1,2,0:T(8,128)} %get-tuple-element.37, f32[12,384]{1,0:T(8,128)} %copy-done.75), kind=kOutput, calls=%fused_computation.241 | convolution fusion | flops 239178624 | bytes 15353856 | tf_op jit(solution)/shard_map/bhqk,bqhe->bkhe/dot_general | solution.py:29
  275.1 4.4 fusion.278
  284.1 42.8 %psum.7 = f32[6,768]{1,0:T(8,128)} all-reduce(f32[6,768]{1,0:T(8,128)} %stack.27), channel_id=1, replica_groups=mesh['data'=32] {'data'}, use_global_device_ids=true, to_apply=%region_27.28 | all-reduce | flops 4608 | bytes 36864 | tf_op jit(solution)/shard_map/psum | solution.py:444
  332.5 550.9 %reduce_tiles.1 = f32[27648,768]{1,0:T(8,128)} custom-call(bf16[384,768]{1,0:T(8,128)(2,1)S(1)} %copy-done.1, bf16[384,2304]{1,0:T(8,128)(2,1)} %maximum_bitcast_fusion.2.refs_1_, bf16[384,768]{1,0:T(8,128)(2,1)S(1)} %copy.96.refs_2_, bf16[384,768]{1,0:T(8,128)(2,1)S(1)} %bitcast.425, bf16[384,768]{1,0:T(8,128)(2,1)S(1)} %copy-done.3, ...), custom_call_target="tpu_custom_call" | custom-call | flops 16307453952 | bytes 169869312 | tf_op jit(solution)/shard_map/reduce_tiles/pallas_call | solution.py:390
  883.4 6.9 spread_tiles.5
  890.3 17.8 %spread_tiles.4 = f32[3,768,2304]{2,1,0:T(8,128)} custom-call(f32[3,12,768,768]{3,2,1,0:T(8,128)} %bitcast.107.src_ref), custom_call_target="tpu_custom_call" | custom-call | tf_op jit(solution)/shard_map/spread_tiles/pallas_call | solution.py:416
  908.1 22.3 %spread_tiles.7 = f32[3,3072,768]{2,1,0:T(8,128)} custom-call(f32[3,12,768,768]{3,2,1,0:T(8,128)} %bitcast.107.src_ref), custom_call_target="tpu_custom_call" | custom-call | tf_op jit(solution)/shard_map/spread_tiles/pallas_call | solution.py:416
  930.4 22.3 %spread_tiles.6 = f32[3,768,3072]{2,1,0:T(8,128)} custom-call(f32[3,12,768,768]{3,2,1,0:T(8,128)} %bitcast.107.src_ref), custom_call_target="tpu_custom_call" | custom-call | tf_op jit(solution)/shard_map/spread_tiles/pallas_call | solution.py:416
  (237 shorter events, 97.8 us)
Async XLA Ops:
  1.9 6.9 copy-start.49
  3.6 17.4 %copy-start.47 = (f32[768]{0:T(1024)}, f32[768]{0:T(1024)S(1)}, u32[]{:S(2)}) copy-start(f32[768]{0:T(1024)S(1)} %get-tuple-element.20) | copy-start | bytes 9220
  21.0 7.3 copy-start.63
  21.0 7.3 copy-start.30
  21.0 7.2 copy-start.51
  21.3 7.0 copy-start.2
  34.6 15.4 %copy-start.32 = (bf16[1,384,768]{2,1,0:T(8,128)(2,1)}, bf16[1,384,768]{2,1,0:T(8,128)(2,1)S(1)}, u32[]{:S(2)}) copy-start(bf16[1,384,768]{2,1,0:T(8,128)(2,1)S(1)} %get-tuple-element.41) | copy-start | bytes 1769476
  52.1 7.3 copy-start.67
  52.1 7.3 copy-start.34
  52.1 7.2 copy-start.55
  52.3 7.0 copy-start.7
  65.7 18.1 %copy-start.36 = (bf16[1,384,768]{2,1,0:T(8,128)(2,1)}, bf16[1,384,768]{2,1,0:T(8,128)(2,1)S(1)}, u32[]{:S(2)}) copy-start(bf16[1,384,768]{2,1,0:T(8,128)(2,1)S(1)} %get-tuple-element.47) | copy-start | bytes 1769476
  71.6 7.3 copy-start.42
  86.1 7.0 copy-start.14
  86.1 7.0 copy-start.15
  106.1 45.2 %copy-start.9 = (bf16[1,384,768]{2,1,0:T(8,128)(2,1)}, bf16[1,384,768]{2,1,0:T(8,128)(2,1)S(1)}, u32[]{:S(2)}) copy-start(bf16[1,384,768]{2,1,0:T(8,128)(2,1)S(1)} %fusion.286) | copy-start | bytes 1769476
  119.1 12.4 %copy-start.43 = (bf16[1,384,768]{1,2,0:T(8,128)(2,1)S(1)}, bf16[1,384,768]{1,2,0:T(8,128)(2,1)}, u32[]{:S(2)}) copy-start(bf16[1,384,768]{1,2,0:T(8,128)(2,1)} %copy-done.42) | copy-start | bytes 1769476
  119.2 12.4 %copy-start.77 = (f32[12,384]{1,0:T(8,128)S(1)}, f32[12,384]{1,0:T(8,128)}, u32[]{:S(2)}) copy-start(f32[12,384]{1,0:T(8,128)} %get-tuple-element.48) | copy-start | bytes 55300
  131.6 14.9 %copy-start.58 = (f32[384]{0:T(512)S(1)}, f32[384]{0:T(512)}, u32[]{:S(2)}) copy-start(f32[384]{0:T(512)} %copy-done.57) | copy-start | bytes 4612
  151.7 6.4 copy-start.35
  151.7 6.4 copy-start.56
  194.2 16.6 %copy-start.23 = (bf16[1,384,768]{2,1,0:T(8,128)(2,1)S(1)}, bf16[1,384,768]{2,1,0:T(8,128)(2,1)}, u32[]{:S(2)}) copy-start(bf16[1,384,768]{2,1,0:T(8,128)(2,1)} %copy.88) | copy-start | bytes 1769476
  194.2 16.6 %copy-start.54 = (f32[384]{0:T(512)S(1)}, f32[384]{0:T(512)}, u32[]{:S(2)}) copy-start(f32[384]{0:T(512)} %copy-done.53) | copy-start | bytes 4612
  216.2 6.4 copy-start.22
  222.5 6.9 copy-start.18
  233.5 7.4 copy-start.20
  258.5 16.6 %copy-start.11 = (bf16[1,384,768]{2,1,0:T(8,128)(2,1)S(1)}, bf16[1,384,768]{2,1,0:T(8,128)(2,1)}, u32[]{:S(2)}) copy-start(bf16[1,384,768]{2,1,0:T(8,128)(2,1)} %param.8) | copy-start | bytes 1769476
  258.5 16.6 %copy-start.46 = (f32[768]{0:T(1024)S(1)}, f32[768]{0:T(1024)}, u32[]{:S(2)}) copy-start(f32[768]{0:T(1024)} %copy-done.45) | copy-start | bytes 9220
  258.5 16.6 %copy-start.50 = (f32[384]{0:T(512)S(1)}, f32[384]{0:T(512)}, u32[]{:S(2)}) copy-start(f32[384]{0:T(512)} %copy-done.49) | copy-start | bytes 4612
  275.1 6.4 copy-start.60
  275.1 6.4 copy-start.12
  279.6 48.7 %copy-start.1 = (bf16[384,768]{1,0:T(8,128)(2,1)S(1)}, bf16[384,768]{1,0:T(8,128)(2,1)}, u32[]{:S(2)}) copy-start(bf16[384,768]{1,0:T(8,128)(2,1)} %copy-done) | copy-start | bytes 1769476
  (46 other events, 188.1 us)

commit v2 on v1

--- a/solution.py
+++ b/solution.py
@@ -13,6 +13,7 @@
 TILES = 12
 SUB = 16
 RING = 16
+SPREAD = 8
 HOP = 2
 MESH_ID = pl.DeviceIdType.MESH
 
@@ -29,53 +30,103 @@
     return jnp.einsum(einsum_spec, lhs_arr, rhs_arr, preferred_element_type=jnp.float32).astype(jnp.bfloat16)
 
 
-def mix_f32(einsum_spec, lhs_arr, rhs_arr):
-    return jnp.einsum(einsum_spec, lhs_arr, rhs_arr, preferred_element_type=jnp.float32)
+def dot_nt(lhs, rhs):
+    return lax.dot_general(lhs, rhs, (((1,), (1,)), ((), ())), preferred_element_type=jnp.float32)
+
+
+def dot_tn(lhs, rhs):
+    return lax.dot_general(lhs, rhs, (((0,), (0,)), ((), ())), preferred_element_type=jnp.float32)
+
+
+def head_probs(q_part, k_pair):
+    scores = dot_nt(q_part, k_pair) * HEAD_DIM ** -0.5
+    rows = lax.broadcasted_iota(jnp.int32, scores.shape, 0)
+    cols = lax.broadcasted_iota(jnp.int32, scores.shape, 1)
+    scores = jnp.where(rows >= cols, scores, -1e30)
+    weights = jnp.exp(scores - jnp.max(scores, axis=-1, keepdims=True))
+    return weights / jnp.sum(weights, axis=-1, keepdims=True)
+
+
+def pair_masks(shape):
+    first = lax.broadcasted_iota(jnp.int32, shape, 1) < HEAD_DIM
+    return first, [jnp.where(first, 1.0, 0.0).astype(jnp.bfloat16), jnp.where(first, 0.0, 1.0).astype(jnp.bfloat16)]
+
+
+def attn_fwd_kernel(q_ref, k_ref, v_ref, o_ref):
+    q_pair, k_pair, v_pair = q_ref[...], k_ref[...], v_ref[...]
+    first, masks = pair_masks(q_pair.shape)
+    outs = [jnp.dot(head_probs(q_pair * mask, k_pair).astype(jnp.bfloat16), v_pair, preferred_element_type=jnp.float32) for mask in masks]
+    o_ref[...] = jnp.where(first, outs[0], outs[1]).astype(jnp.bfloat16)
+
+
+def attn_bwd_kernel(q_ref, k_ref, v_ref, do_ref, dqkv_ref):
+    pair = pl.program_id(0)
+    q_pair, k_pair, v_pair, do_pair = q_ref[...], k_ref[...], v_ref[...], do_ref[...]
+    first, masks = pair_masks(q_pair.shape)
+    grads = []
+    for mask in masks:
+        prob = head_probs(q_pair * mask, k_pair)
+        grad_prob = dot_nt(do_pair * mask, v_pair)
+        grad_score = (prob * (grad_prob - jnp.sum(prob * grad_prob, axis=-1, keepdims=True)) * HEAD_DIM ** -0.5).astype(jnp.bfloat16)
+        grads.append((
+            jnp.dot(grad_score, k_pair, preferred_element_type=jnp.float32),
+            dot_tn(grad_score, q_pair),
+            dot_tn(prob.astype(jnp.bfloat16), do_pair),
+        ))
+    for part_idx in range(3):
+        cols = pl.ds(pl.multiple_of(part_idx * WIDTH + pair * 2 * HEAD_DIM, 2 * HEAD_DIM), 2 * HEAD_DIM)
+        dqkv_ref[:, cols] = jnp.where(first, grads[0][part_idx], grads[1][part_idx]).astype(jnp.bfloat16)
+
+
+def attn_specs(rows, count):
+    pairs = WIDTH // (2 * HEAD_DIM)
+    return pairs, [pl.BlockSpec((rows, 2 * HEAD_DIM), lambda h, lo=lo * pairs: (0, lo + h)) for lo in range(count)]
+
+
+def attention(qkv):
+    rows = qkv.shape[0]
+    pairs, specs = attn_specs(rows, 3)
+    return pl.pallas_call(
+        attn_fwd_kernel, grid=(pairs,), in_specs=specs, out_specs=attn_specs(rows, 1)[1][0],
+        out_shape=jax.ShapeDtypeStruct((rows, WIDTH), jnp.bfloat16), name='attn_fwd',
+    )(qkv, qkv, qkv)
+
+
+def attention_grad(qkv, grad_attn):
+    rows = qkv.shape[0]
+    pairs, specs = attn_specs(rows, 3)
+    return pl.pallas_call(
+        attn_bwd_kernel, grid=(pairs,), in_specs=specs + attn_specs(rows, 1)[1], out_specs=pl.BlockSpec((rows, 3 * WIDTH), lambda h: (0, 0)),
+        out_shape=jax.ShapeDtypeStruct((rows, 3 * WIDTH), jnp.bfloat16), name='attn_bwd',
+    )(qkv, qkv, qkv, grad_attn)
 
 
 def block_forward(x_blk, gain_a, gain_b, w_qkv, w_out, w_up):
-    n_batch, seq_len, width = x_blk.shape
-    head_shape = (n_batch, seq_len, width // HEAD_DIM, HEAD_DIM)
     norm_a, norm_a_back = jax.vjp(rms_gain, x_blk.astype(jnp.float32), gain_a)
     u_one = norm_a.astype(jnp.bfloat16)
-    qkv_lo = mix_lo('bsd,de->bse', u_one, w_qkv)
-    q_all = qkv_lo[:, :, :width].reshape(head_shape)
-    k_all = qkv_lo[:, :, width:2 * width].reshape(head_shape)
-    v_all = qkv_lo[:, :, 2 * width:].reshape(head_shape)
-    scores = mix_f32('bqhe,bkhe->bhqk', q_all, k_all) * HEAD_DIM ** -0.5
-    causal = jnp.arange(seq_len)[:, None] >= jnp.arange(seq_len)[None, :]
-    prob_full = jax.nn.softmax(jnp.where(causal, scores, -1e30), axis=-1)
-    prob_lo = prob_full.astype(jnp.bfloat16)
-    attn_out = mix_lo('bhqk,bkhe->bqhe', prob_lo, v_all).reshape(n_batch, seq_len, width)
-    hidden = x_blk + mix_lo('bsd,de->bse', attn_out, w_out)
+    qkv_lo = mix_lo('sd,de->se', u_one, w_qkv)
+    attn_out = attention(qkv_lo)
+    hidden = x_blk + mix_lo('sd,de->se', attn_out, w_out)
     norm_b, norm_b_back = jax.vjp(rms_gain, hidden.astype(jnp.float32), gain_b)
     u_two = norm_b.astype(jnp.bfloat16)
-    pre_lo = mix_lo('bsd,df->bsf', u_two, w_up)
+    pre_lo = mix_lo('sd,df->sf', u_two, w_up)
     act_f, gelu_back = jax.vjp(gelu_tanh, pre_lo.astype(jnp.float32))
     act_lo = act_f.astype(jnp.bfloat16)
-    saved_vals = (norm_a_back, u_one, q_all, k_all, v_all, prob_full, prob_lo, attn_out, norm_b_back, u_two, gelu_back, act_lo)
+    saved_vals = (norm_a_back, u_one, qkv_lo, attn_out, norm_b_back, u_two, gelu_back, act_lo)
     return hidden, act_lo, saved_vals
 
 
 def block_backward(grad_blk, saved_vals, w_qkv, w_out, w_up, w_down):
-    (norm_a_back, u_one, q_all, k_all, v_all, prob_full, prob_lo, attn_out, norm_b_back, u_two, gelu_back, act_lo) = saved_vals
-    n_batch, seq_len, width = grad_blk.shape
-    head_shape = (n_batch, seq_len, width // HEAD_DIM, HEAD_DIM)
-    grad_act = mix_lo('bsd,fd->bsf', grad_blk, w_down)
+    (norm_a_back, u_one, qkv_lo, attn_out, norm_b_back, u_two, gelu_back, act_lo) = saved_vals
+    grad_act = mix_lo('sd,fd->sf', grad_blk, w_down)
     (grad_pre_f,) = gelu_back(grad_act.astype(jnp.float32))
     grad_pre = grad_pre_f.astype(jnp.bfloat16)
-    grad_u_two = mix_lo('bsf,df->bsd', grad_pre, w_up)
+    grad_u_two = mix_lo('sf,df->sd', grad_pre, w_up)
     grad_h_norm, grad_gain_b = norm_b_back(grad_u_two.astype(jnp.float32))
     grad_hidden = (grad_blk.astype(jnp.float32) + grad_h_norm).astype(jnp.bfloat16)
-    grad_attn = mix_lo('bse,de->bsd', grad_hidden, w_out).reshape(head_shape)
-    grad_probs = mix_f32('bqhe,bkhe->bhqk', grad_attn, v_all)
-    grad_scores = (prob_full * (grad_probs - jnp.sum(prob_full * grad_probs, axis=-1, keepdims=True)) * HEAD_DIM ** -0.5).astype(jnp.bfloat16)
-    grad_v = mix_lo('bhqk,bqhe->bkhe', prob_lo, grad_attn)
-    grad_q = mix_lo('bhqk,bkhe->bqhe', grad_scores, k_all)
-    grad_k = mix_lo('bhqk,bqhe->bkhe', grad_scores, q_all)
-    flat_shape = (n_batch, seq_len, width)
-    grad_qkv = jnp.concatenate([grad_q.reshape(flat_shape), grad_k.reshape(flat_shape), grad_v.reshape(flat_shape)], axis=-1)
-    grad_u_one = mix_lo('bse,de->bsd', grad_qkv, w_qkv)
+    grad_attn = mix_lo('se,de->sd', grad_hidden, w_out)
+    grad_qkv = attention_grad(qkv_lo, grad_attn)
+    grad_u_one = mix_lo('se,de->sd', grad_qkv, w_qkv)
     grad_x_norm, grad_gain_a = norm_a_back(grad_u_one.astype(jnp.float32))
     grad_x_blk = (grad_hidden.astype(jnp.float32) + grad_x_norm).astype(jnp.bfloat16)
     factors = (u_one, grad_qkv, attn_out, grad_hidden, u_two, grad_pre, act_lo, grad_blk)
@@ -95,7 +146,7 @@
     reduce_body(n_tile, n_dev, refs[:n_factor], *refs[n_factor:])
 
 
-def reduce_body(n_tile, n_dev, f_refs, g_ref, fa, fb, part, ra, acc, rzb, rza, rb, fin,
+def reduce_body(n_tile, n_dev, f_refs, gain_ref, g_ref, gain_out, gs, gr, gz, gs_s, gs_r, gz_s, gz_r, fa, fb, part, ra, acc, rzb, rza, rb, fin,
                   fl_a, fl_b, fs_a, fs_b, fr_a, fr_b,
                   ra_s, ra_r, z_s, zb_r, za_r, b_s, b_r, bag_s, bag_r, loc, bc_r, up_s, dn_s, aag_s, aag_r, p1_s, p1_r, p2_s, p2_r):
     toks = f_refs[0].shape[0]
@@ -114,15 +165,10 @@
     for dev in (x_dev, y_dev, pair_dev):
         pl.semaphore_signal(barrier, inc=1, device_id=(dev,), device_id_type=MESH_ID)
 
-    @pl.when(my_z < top_z)
-    def _():
-        pl.semaphore_signal(barrier, inc=1, device_id=(up_dev,), device_id_type=MESH_ID)
-
-    @pl.when(my_z > 0)
-    def _():
-        pl.semaphore_signal(barrier, inc=1, device_id=(dn_dev,), device_id_type=MESH_ID)
-
-    pl.semaphore_wait(barrier, 3 + jnp.where(my_z < top_z, 1, 0) + jnp.where(my_z > 0, 1, 0))
+    z_devs = [me + 8 * ((my_z + dist) % (top_z + 1) - my_z) for dist in range(1, top_z + 1)]
+    for dev in z_devs:
+        pl.semaphore_signal(barrier, inc=1, device_id=(dev,), device_id_type=MESH_ID)
+    pl.semaphore_wait(barrier, 3 + top_z)
 
     def remote(src, dst, send_sem, recv_sem, dev):
         return pltpu.make_async_remote_copy(src_ref=src, dst_ref=dst, send_sem=send_sem, recv_sem=recv_sem, device_id=(dev,), device_id_type=MESH_ID)
@@ -341,11 +387,48 @@
         stages += [stage_swap, stage_done]
         return stages
 
+    gain_devs = (pair_dev, x_dev, y_dev)
+
+    def gain_copy(hop):
+        return remote(gs.at[hop], gr.at[hop], gs_s.at[hop], gs_r.at[hop], gain_devs[hop])
+
+    def gain_line(dist, slot):
+        return remote(gs.at[3], gz.at[slot], gz_s.at[dist], gz_r.at[slot], z_devs[dist])
+
+    def gain_steps(t):
+        @pl.when(t == 0)
+        def _():
+            gs[0] = gain_ref[...]
+            gain_copy(0).start()
+
+        for hop in range(1, 4):
+            @pl.when(t == 4 * hop)
+            def _():
+                gain_copy(hop - 1).wait()
+                gs[hop] = gs[hop - 1] + gr[hop - 1]
+                if hop < 3:
+                    gain_copy(hop).start()
+                else:
+                    gz[my_z] = gs[hop]
+                    for dist in range(top_z):
+                        gain_line(dist, my_z).start()
+
+        @pl.when(t == 16)
+        def _():
+            for dist in range(top_z):
+                gain_line(dist, my_z).wait_send()
+                gain_line(dist, (my_z + dist + 1) % (top_z + 1)).wait_recv()
+            total = gz[0]
+            for slot in range(1, top_z + 1):
+                total = total + gz[slot]
+            gain_out[...] = total * (1.0 / n_dev)
+
     streams = [stream_stages(0), stream_stages(1)]
     n_stage = len(streams[0])
 
     def step(t, carry):
         tile = t // per_tile
+        gain_steps(t)
 
         for stage_idx in reversed(range(1, n_stage)):
             u = t - HOP * stage_idx
@@ -380,7 +463,7 @@
     lax.fori_loop(0, n_unit + HOP * (n_stage - 1), step, 0)
 
 
-def reduce_tiles(factors, n_tile, n_dev):
+def reduce_tiles(factors, gains, n_tile, n_dev):
     toks = factors[0].shape[0]
     half = WIDTH // 2
     f32, bf16 = jnp.float32, jnp.bfloat16
@@ -389,10 +472,14 @@
     flops = n_tile * 2 * half * 2 * toks * WIDTH
     return pl.pallas_call(
         functools.partial(reduce_kernel, n_tile, n_dev),
-        out_shape=jax.ShapeDtypeStruct((n_tile * WIDTH, WIDTH), f32),
-        in_specs=[pl.BlockSpec(memory_space=pl.ANY)] * len(factors),
-        out_specs=pl.BlockSpec(memory_space=pl.ANY),
+        out_shape=(jax.ShapeDtypeStruct((n_tile * WIDTH, WIDTH), f32), jax.ShapeDtypeStruct(gains.shape, f32)),
+        in_specs=[pl.BlockSpec(memory_space=pl.ANY)] * len(factors) + [pl.BlockSpec(memory_space=pltpu.VMEM)],
+        out_specs=(pl.BlockSpec(memory_space=pl.ANY), pl.BlockSpec(memory_space=pltpu.VMEM)),
         scratch_shapes=[
+            pltpu.VMEM((4,) + gains.shape, f32),
+            pltpu.VMEM((3,) + gains.shape, f32),
+            pltpu.VMEM((n_dev // 8,) + gains.shape, f32),
+            dma((3,)), dma((3,)), dma((n_dev // 8 - 1,)), dma((n_dev // 8,)),
             pltpu.VMEM((4, 2 * toks, half), bf16),
             pltpu.VMEM((4, 2 * toks, WIDTH), bf16),
             pltpu.VMEM((2, half, WIDTH), f32),
@@ -403,22 +490,49 @@
         compiler_params=pltpu.CompilerParams(collective_id=0, has_side_effects=True, vmem_limit_bytes=48 * 1024 * 1024),
         cost_estimate=pl.CostEstimate(flops=flops, bytes_accessed=n_tile * WIDTH * WIDTH * 8, transcendentals=0),
         name='reduce_tiles',
-    )(*factors)
-
-
-def copy_block(src_ref, dst_ref):
-    dst_ref[0] = src_ref[0, 0]
-
-
-def spread_tiles(tiles, first, count, down=False):
-    n_layers = tiles.shape[0]
-    shape = (n_layers, count * WIDTH, WIDTH) if down else (n_layers, WIDTH, count * WIDTH)
+    )(*factors, gains)
+
+
+def spread_kernel(n_layers, src_ref, qkv_ref, out_ref, up_ref, down_ref, buf, read_sem, write_sem):
+    moves = []
+    for layer in range(n_layers):
+        for j in range(TILES):
+            if j < 3:
+                dst = qkv_ref.at[layer, :, pl.ds(j * WIDTH, WIDTH)]
+            elif j < 4:
+                dst = out_ref.at[layer]
+            elif j < 8:
+                dst = up_ref.at[layer, :, pl.ds((j - 4) * WIDTH, WIDTH)]
+            else:
+                dst = down_ref.at[layer, pl.ds((j - 8) * WIDTH, WIDTH)]
+            slot = len(moves) % SPREAD
+            moves.append((pltpu.make_async_copy(src_ref.at[pl.ds((layer * TILES + j) * WIDTH, WIDTH)], buf.at[slot], read_sem.at[slot]),
+                          pltpu.make_async_copy(buf.at[slot], dst, write_sem.at[slot])))
+    ahead = SPREAD // 2
+    for read, _ in moves[:ahead]:
+        read.start()
+    for idx, (read, write) in enumerate(moves):
+        if idx >= ahead:
+            moves[idx - ahead][1].wait()
+        if idx + ahead < len(moves):
+            moves[idx + ahead][0].start()
+        read.wait()
+        write.start()
+    for _, write in moves[-ahead:]:
+        write.wait()
+
+
+def spread_tiles(tiles, n_layers):
+    f32 = jnp.float32
+    anyspace = pl.BlockSpec(memory_space=pl.ANY)
+    shapes = ((WIDTH, 3 * WIDTH), (WIDTH, WIDTH), (WIDTH, 4 * WIDTH), (4 * WIDTH, WIDTH))
     return pl.pallas_call(
-        copy_block,
-        grid=(n_layers, count),
-        out_shape=jax.ShapeDtypeStruct(shape, tiles.dtype),
-        in_specs=[pl.BlockSpec((1, 1, WIDTH, WIDTH), lambda layer, j: (layer, first + j, 0, 0))],
-        out_specs=pl.BlockSpec((1, WIDTH, WIDTH), (lambda layer, j: (layer, j, 0)) if down else (lambda layer, j: (layer, 0, j))),
+        functools.partial(spread_kernel, n_layers),
+        out_shape=tuple(jax.ShapeDtypeStruct((n_layers,) + shape, f32) for shape in shapes),
+        in_specs=[anyspace],
+        out_specs=(anyspace,) * 4,
+        scratch_shapes=[pltpu.VMEM((SPREAD, WIDTH, WIDTH), f32), pltpu.SemaphoreType.DMA((SPREAD,)), pltpu.SemaphoreType.DMA((SPREAD,))],
+        compiler_params=pltpu.CompilerParams(vmem_limit_bytes=32 * 1024 * 1024),
         name='spread_tiles',
     )(tiles)
 
@@ -428,24 +542,21 @@
 
     def local_step(x_loc, grad_y_loc, gain_one, gain_two, w_qkv, w_out, w_up, w_down):
         n_layers = w_qkv.shape[0]
-        hidden_x = x_loc
+        hidden_x = x_loc[0]
         saved_all = []
         for layer_idx in range(n_layers):
             hidden, act_lo, saved_vals = block_forward(hidden_x, gain_one[layer_idx], gain_two[layer_idx], w_qkv[layer_idx], w_out[layer_idx], w_up[layer_idx])
             saved_all.append(saved_vals)
             if layer_idx + 1 < n_layers:
-                hidden_x = hidden + mix_lo('bsf,fd->bsd', act_lo, w_down[layer_idx])
-        grad_cur = grad_y_loc
+                hidden_x = hidden + mix_lo('sf,fd->sd', act_lo, w_down[layer_idx])
+        grad_cur = grad_y_loc[0]
         all_factors = [None] * n_layers
         gain_grads = [None] * (2 * n_layers)
         for layer_idx in reversed(range(n_layers)):
-            grad_cur, gain_grads[layer_idx], gain_grads[n_layers + layer_idx], factors = block_backward(grad_cur, saved_all[layer_idx], w_qkv[layer_idx], w_out[layer_idx], w_up[layer_idx], w_down[layer_idx])
-            all_factors[layer_idx] = [factor.reshape(factor.shape[1:]) for factor in factors]
-        gain_sum = lax.psum(jnp.stack(gain_grads), 'data') / n_dev
-        tiles = reduce_tiles([factor for layer in all_factors for factor in layer], n_layers * TILES, n_dev).reshape(n_layers, TILES, WIDTH, WIDTH)
-
-        return (grad_cur, gain_sum[:n_layers], gain_sum[n_layers:], spread_tiles(tiles, 0, 3), spread_tiles(tiles, 3, 1), spread_tiles(tiles, 4, 4),
-                spread_tiles(tiles, 8, 4, down=True))
+            grad_cur, gain_grads[layer_idx], gain_grads[n_layers + layer_idx], all_factors[layer_idx] = block_backward(grad_cur, saved_all[layer_idx], w_qkv[layer_idx], w_out[layer_idx], w_up[layer_idx], w_down[layer_idx])
+        gains = jnp.stack(gain_grads + [jnp.zeros_like(gain_grads[0])] * (-2 * n_layers % 8))
+        tiles, gain_sum = reduce_tiles([factor for layer in all_factors for factor in layer], gains, n_layers * TILES, n_dev)
+        return (grad_cur[None], gain_sum[:n_layers], gain_sum[n_layers:2 * n_layers]) + tuple(spread_tiles(tiles, n_layers))
 
     batch_spec = P('data')
     full_spec = P()

time: 958 us -> 814 us (0.85)
  matrix products: 238 us -> 113 us
  Pallas kernels: 620 us -> 671 us
  blocking collectives: 42.8 us -> 0 us
  local copies, waits for them, and re-layouts: 38.6 us -> 11.3 us
    dot_general x35 -> x23, matrix products: 206 us -> 113 us  [mix_lo(): jnp.einsum(einsum_spec, lhs_arr, rhs_arr, preferred_element_type=jnp.floa...]
    pallas_call x4 -> x7, Pallas kernels: 69.2 us -> 116 us  [the longest x1 56.1 us: spread_tiles(): pl.pallas_call(functools.partial(spread_kernel, n_layers), out_shape=tupl...]
    psum x1 -> x0, blocking collectives: 42.8 us -> none  [local_step(): gain_sum = lax.psum(jnp.stack(gain_grads), 'data') / n_dev]
    sub x3 -> x0, matrix products: 17.5 us -> none  [block_forward(): prob_full = jax.nn.softmax(jnp.where(causal, scores, -1e+30), axis=-1)]
    dot_general x3 -> x0, matrix products: 14.4 us -> none  [mix_f32(): jnp.einsum(einsum_spec, lhs_arr, rhs_arr, preferred_element_type=jnp.floa...]
    reshape x9 -> x6, local copies, waits for them, and re-layouts: 16.6 us -> 3.54 us  [rms_gain(): rows_f * lax.rsqrt(jnp.mean(rows_f * rows_f, axis=-1, keepdims=True) + NO...]
where the time goes in v2:
time: 814 us; the launch traced here: 805 us
  Pallas kernels  671 us (82%)
  matrix products  113 us (14%)
  local copies, waits for them, and re-layouts  11.3 us (1%)
  other arithmetic  8.4 us (1%)
    pallas_call x1, Pallas kernels, reduce_tiles(): pl.pallas_call(functools.partial(reduce_kernel, n_tile, n_dev), out_shape...  555 us
    dot_general x23, matrix products, mix_lo(): jnp.einsum(einsum_spec, lhs_arr, rhs_arr, preferred_element_type=jnp.floa...  113 us
    pallas_call x1, Pallas kernels, spread_tiles(): pl.pallas_call(functools.partial(spread_kernel, n_layers), out_shape=tupl...  56.1 us
    pallas_call x3, Pallas kernels, attention_grad(): pl.pallas_call(attn_bwd_kernel, grid=(pairs,), in_specs=specs + attn_spec...  35 us
    pallas_call x3, Pallas kernels, attention(): pl.pallas_call(attn_fwd_kernel, grid=(pairs,), in_specs=specs, out_specs=...  24.6 us

profile of v2, /device:TPU:0, one launch (start us, length us, event | category | flops | bytes accessed | tf_op | source)
XLA Modules:
  0.0 805.0 jit_solution(4697808719176196881)
XLA Ops:
  3.6 5.0 convolution_convert_fusion.2.q_ref.k_ref.v_ref
  8.7 8.1 %attn_fwd.3.refs_2_ = bf16[384,768]{1,0:T(8,128)(2,1)} custom-call(bf16[384,2304]{1,0:T(8,128)(2,1)} %convolution_convert_fusion.2.q_ref.k_ref.v_ref, bf16[384,2304]{1,0:T(8,128)(2,1)} %convolution_convert_fusion.2.q_ref.k_ref.v_ref, bf16[384,2304]{1,0:T(8,128)(2,1)} %convolution_convert_fusion.2.q_ref.k_ref.v_ref), custom_call_target="tpu_custom_call" | custom-call | tf_op jit(solution)/shard_map/attn_fwd/pallas_call | solution.py:89
  16.8 2.2 fusion.176
  19.2 6.9 fusion.18
  26.1 6.3 fusion.178
  32.7 5.0 convolution_convert_fusion.1.q_ref.k_ref.v_ref
  37.7 8.5 %attn_fwd.4.refs_10_ = bf16[384,768]{1,0:T(8,128)(2,1)} custom-call(bf16[384,2304]{1,0:T(8,128)(2,1)} %convolution_convert_fusion.1.q_ref.k_ref.v_ref, bf16[384,2304]{1,0:T(8,128)(2,1)} %convolution_convert_fusion.1.q_ref.k_ref.v_ref, bf16[384,2304]{1,0:T(8,128)(2,1)} %convolution_convert_fusion.1.q_ref.k_ref.v_ref), custom_call_target="tpu_custom_call" | custom-call | tf_op jit(solution)/shard_map/attn_fwd/pallas_call | solution.py:89
  46.1 2.2 fusion.180
  48.6 6.9 fusion.24
  55.5 6.3 fusion.182
  62.0 5.0 convolution_convert_fusion.q_ref.k_ref.v_ref
  67.0 8.0 attn_fwd.5.refs_18_
  75.1 2.2 fusion.184
  77.5 7.0 fusion.32
  84.5 6.3 fusion.5.refs_21_
  90.8 5.4 fusion.156
  98.0 3.0 convolution_convert_fusion.5.do_ref
  100.9 11.6 %attn_bwd.3.refs_17_ = bf16[384,2304]{1,0:T(8,128)(2,1)} custom-call(bf16[384,2304]{1,0:T(8,128)(2,1)} %convolution_convert_fusion.q_ref.k_ref.v_ref, bf16[384,2304]{1,0:T(8,128)(2,1)} %convolution_convert_fusion.q_ref.k_ref.v_ref, bf16[384,2304]{1,0:T(8,128)(2,1)} %convolution_convert_fusion.q_ref.k_ref.v_ref, bf16[384,768]{1,0:T(8,128)(2,1)} %convolution_convert_fusion.5.do_ref), custom_call_target="tpu_custom_call" | custom-call | tf_op jit(solution)/shard_map/attn_bwd/pallas_call | solution.py:98
  112.5 4.4 fusion.157
  118.0 6.3 fusion.8.refs_13_
  124.4 5.4 fusion.158
  130.8 2.7 convolution_convert_fusion.4.do_ref
  133.6 11.6 %attn_bwd.4.refs_9_ = bf16[384,2304]{1,0:T(8,128)(2,1)} custom-call(bf16[384,2304]{1,0:T(8,128)(2,1)} %convolution_convert_fusion.1.q_ref.k_ref.v_ref, bf16[384,2304]{1,0:T(8,128)(2,1)} %convolution_convert_fusion.1.q_ref.k_ref.v_ref, bf16[384,2304]{1,0:T(8,128)(2,1)} %convolution_convert_fusion.1.q_ref.k_ref.v_ref, ...), custom_call_target="tpu_custom_call" | custom-call | tf_op jit(solution)/shard_map/attn_bwd/pallas_call | solution.py:98
  145.2 4.4 fusion.159
  150.7 6.1 fusion.11.refs_5_
  156.8 5.4 fusion.160
  163.3 2.7 convolution_convert_fusion.3.do_ref
  166.0 11.8 %attn_bwd.5.refs_1_ = bf16[384,2304]{1,0:T(8,128)(2,1)} custom-call(bf16[384,2304]{1,0:T(8,128)(2,1)} %convolution_convert_fusion.2.q_ref.k_ref.v_ref, bf16[384,2304]{1,0:T(8,128)(2,1)} %convolution_convert_fusion.2.q_ref.k_ref.v_ref, bf16[384,2304]{1,0:T(8,128)(2,1)} %convolution_convert_fusion.2.q_ref.k_ref.v_ref, ...), custom_call_target="tpu_custom_call" | custom-call | tf_op jit(solution)/shard_map/attn_bwd/pallas_call | solution.py:98
  177.9 5.8 fusion.161
  186.3 2.6 fusion.155
  192.8 555.1 %reduce_tiles.1 = (f32[27648,768]{1,0:T(8,128)}, f32[8,768]{1,0:T(8,128)S(1)}) custom-call(bf16[384,768]{1,0:T(8,128)(2,1)S(1)} %get-tuple-element.37.refs_0_, bf16[384,2304]{1,0:T(8,128)(2,1)} %attn_bwd.5.refs_1_, bf16[384,768]{1,0:T(8,128)(2,1)S(1)} %copy-done, bf16[384,768]{1,0:T(8,128)(2,1)S(1)} %fusion.171.refs_3_, bf16[384,768]{1,0:T(8,128)(2,1)S(1)} %copy-done.3, ...), custom_call_target="tpu_custom_call" | custom-call | flops 16307453952 | bytes 169869312 | tf_op jit(solution)/shard_map/reduce_tiles/pallas_call | solution.py:473
  748.5 56.1 %spread_tiles.1 = (f32[3,768,2304]{2,1,0:T(8,128)}, f32[3,768,768]{2,1,0:T(8,128)}, f32[3,768,3072]{2,1,0:T(8,128)}, f32[3,3072,768]{2,1,0:T(8,128)}) custom-call(f32[27648,768]{1,0:T(8,128)} %get-tuple-element.14.src_ref), custom_call_target="tpu_custom_call" | custom-call | tf_op jit(solution)/shard_map/spread_tiles/pallas_call | solution.py:529
  (124 shorter events, 17.1 us)
Async XLA Ops:
  1.9 6.8 copy-start.24
  1.9 6.8 copy-start.36
  2.8 5.9 copy-start.26
  3.6 87.2 %copy-start.14 = (f32[768]{0:T(1024)}, f32[768]{0:T(1024)S(1)}, u32[]{:S(2)}) copy-start(f32[768]{0:T(1024)S(1)} %get-tuple-element.31) | copy-start | bytes 9220
  8.7 8.1 %copy-start.9 = (bf16[1,384,768]{2,1,0:T(8,128)(2,1)S(1)}, bf16[1,384,768]{2,1,0:T(8,128)(2,1)}, u32[]{:S(2)}) copy-start(bf16[1,384,768]{2,1,0:T(8,128)(2,1)} %param.8) | copy-start | bytes 1769476
  19.0 7.2 copy-start.28
  19.0 7.1 copy-start.15
  19.2 6.9 copy-start.2
  26.1 6.3 copy-start.41
  48.3 7.2 copy-start.32
  48.3 7.2 copy-start.19
  48.5 6.9 copy-start.6
  55.5 6.3 copy-start.43
  77.5 7.0 copy-start.12
  77.5 7.0 copy-start.13
  90.8 5.4 copy-start.38
  98.0 19.6 %copy-start.10 = (bf16[384,768]{1,0:T(8,128)(2,1)}, bf16[384,768]{1,0:T(8,128)(2,1)S(1)}, u32[]{:S(2)}) copy-start(bf16[384,768]{1,0:T(8,128)(2,1)S(1)} %fusion.163.refs_19_) | copy-start | bytes 1769476
  100.9 11.6 %copy-start.22 = (f32[384]{0:T(512)S(1)}, f32[384]{0:T(512)}, u32[]{:S(2)}) copy-start(f32[384]{0:T(512)} %copy-done.21) | copy-start | bytes 4612
  112.5 5.5 copy-start.44
  118.0 6.4 copy-start.20
  124.4 5.4 copy-start.39
  124.4 6.0 copy-start.33
  133.6 11.6 %copy-start.18 = (f32[384]{0:T(512)S(1)}, f32[384]{0:T(512)}, u32[]{:S(2)}) copy-start(f32[384]{0:T(512)} %copy-done.17) | copy-start | bytes 4612
  145.2 5.4 copy-start.42
  150.6 6.1 copy-start.16
  156.8 5.4 copy-start.40
  156.8 6.0 copy-start.29
  166.0 11.8 %copy-start.27 = (f32[768]{0:T(1024)S(1)}, f32[768]{0:T(1024)}, u32[]{:S(2)}) copy-start(f32[768]{0:T(1024)} %copy-done.26) | copy-start | bytes 9220
  166.0 11.8 %copy-start.37 = (f32[384]{0:T(512)S(1)}, f32[384]{0:T(512)}, u32[]{:S(2)}) copy-start(f32[384]{0:T(512)} %copy-done.36) | copy-start | bytes 4612
  177.9 7.8 copy-start.25
  177.9 11.0 %copy-start = (bf16[384,768]{1,0:T(8,128)(2,1)S(1)}, bf16[384,768]{1,0:T(8,128)(2,1)}, u32[]{:S(2)}) copy-start(bf16[384,768]{1,0:T(8,128)(2,1)} %attn_fwd.3.refs_2_) | copy-start | bytes 1769476
  177.9 11.0 %copy-start.1 = (bf16[384,768]{1,0:T(8,128)(2,1)S(1)}, bf16[384,768]{1,0:T(8,128)(2,1)}, u32[]{:S(2)}) copy-start(bf16[384,768]{1,0:T(8,128)(2,1)} %attn_fwd.4.refs_10_) | copy-start | bytes 1769476
  (13 other events, 49.9 us)

commit v3 on v2

--- a/solution.py
+++ b/solution.py
@@ -1,4 +1,5 @@
 import functools
+import math
 
 import jax
 import jax.numpy as jnp
@@ -14,6 +15,7 @@
 SUB = 16
 RING = 16
 SPREAD = 8
+PIECES = 12
 HOP = 2
 MESH_ID = pl.DeviceIdType.MESH
 
@@ -59,9 +61,7 @@
     o_ref[...] = jnp.where(first, outs[0], outs[1]).astype(jnp.bfloat16)
 
 
-def attn_bwd_kernel(q_ref, k_ref, v_ref, do_ref, dqkv_ref):
-    pair = pl.program_id(0)
-    q_pair, k_pair, v_pair, do_pair = q_ref[...], k_ref[...], v_ref[...], do_ref[...]
+def pair_grads(q_pair, k_pair, v_pair, do_pair):
     first, masks = pair_masks(q_pair.shape)
     grads = []
     for mask in masks:
@@ -73,9 +73,14 @@
             dot_tn(grad_score, q_pair),
             dot_tn(prob.astype(jnp.bfloat16), do_pair),
         ))
+    return [jnp.where(first, grads[0][idx], grads[1][idx]).astype(jnp.bfloat16) for idx in range(3)]
+
+
+def attn_bwd_kernel(q_ref, k_ref, v_ref, do_ref, dqkv_ref):
+    pair = pair_grads(q_ref[...], k_ref[...], v_ref[...], do_ref[...])
     for part_idx in range(3):
-        cols = pl.ds(pl.multiple_of(part_idx * WIDTH + pair * 2 * HEAD_DIM, 2 * HEAD_DIM), 2 * HEAD_DIM)
-        dqkv_ref[:, cols] = jnp.where(first, grads[0][part_idx], grads[1][part_idx]).astype(jnp.bfloat16)
+        cols = pl.ds(pl.multiple_of(part_idx * WIDTH + pl.program_id(0) * 2 * HEAD_DIM, 2 * HEAD_DIM), 2 * HEAD_DIM)
+        dqkv_ref[:, cols] = pair[part_idx]
 
 
 def attn_specs(rows, count):
@@ -113,7 +118,7 @@
     act_f, gelu_back = jax.vjp(gelu_tanh, pre_lo.astype(jnp.float32))
     act_lo = act_f.astype(jnp.bfloat16)
     saved_vals = (norm_a_back, u_one, qkv_lo, attn_out, norm_b_back, u_two, gelu_back, act_lo)
-    return hidden, act_lo, saved_vals
+    return hidden, act_lo, saved_vals, (u_one, attn_out, u_two, act_lo), (x_blk, hidden, pre_lo, qkv_lo)
 
 
 def block_backward(grad_blk, saved_vals, w_qkv, w_out, w_up, w_down):
@@ -141,14 +146,185 @@
     return tiles
 
 
-def reduce_kernel(n_tile, n_dev, *refs):
-    n_factor = 8 * (-(-n_tile // TILES))
-    reduce_body(n_tile, n_dev, refs[:n_factor], *refs[n_factor:])
-
-
-def reduce_body(n_tile, n_dev, f_refs, gain_ref, g_ref, gain_out, gs, gr, gz, gs_s, gs_r, gz_s, gz_r, fa, fb, part, ra, acc, rzb, rza, rb, fin,
-                  fl_a, fl_b, fs_a, fs_b, fr_a, fr_b,
-                  ra_s, ra_r, z_s, zb_r, za_r, b_s, b_r, bag_s, bag_r, loc, bc_r, up_s, dn_s, aag_s, aag_r, p1_s, p1_r, p2_s, p2_r):
+def norm_grad(rows, gain, grad_out):
+    scale = lax.rsqrt(jnp.mean(rows * rows, axis=-1, keepdims=True) + NORM_EPS)
+    grad_gain = jnp.sum(grad_out * rows * scale, axis=0, keepdims=True)
+    grad_unit = grad_out * gain
+    grad_rows = grad_unit * scale - rows * (scale * scale * scale) * jnp.mean(rows * grad_unit, axis=-1, keepdims=True)
+    return grad_rows, grad_gain
+
+
+def gelu_slope(z):
+    const = (2.0 / math.pi) ** 0.5
+    curve = jnp.tanh(const * (z + 0.044715 * (z * z * z)))
+    return 0.5 * (1.0 + curve) + 0.5 * z * (1.0 - curve * curve) * const * (1.0 + 3.0 * 0.044715 * (z * z))
+
+
+def backward_pieces(n_layers, saved, weights, gain_one, gain_two, grads_hbm, dx_hbm, grad_x, gs, vm, load, store):
+    w_qkv, w_out, w_up, w_down = weights
+    dqkv_hbm, dh_hbm, dz_hbm = grads_hbm
+    w2, w1, zb, hb, wo, qkvb, wq, xb, dz, dh, dqkv, dy, do, acc = vm
+    n_low = n_layers - 1
+
+    def cols(j):
+        return pl.ds(pl.multiple_of(j * WIDTH, WIDTH), WIDTH)
+
+    def weight_loads(low, j):
+        layer, slot = n_layers - 2 - low, j % 2
+        return (pltpu.make_async_copy(w_down.at[layer, cols(j)], w2.at[slot], load.at[slot]),
+                pltpu.make_async_copy(w_up.at[layer, :, cols(j)], w1.at[slot], load.at[2 + slot]))
+
+    def saved_load(kind, low, src_cols, dst, sem, act):
+        for which in range(n_low):
+            src = saved[which][kind] if src_cols is None else saved[which][kind].at[:, src_cols]
+
+            @pl.when(low == which)
+            def _():
+                getattr(pltpu.make_async_copy(src, dst, sem), act)()
+
+    def mlp_loads(low, j, act):
+        for copy in weight_loads(low, j):
+            getattr(copy, act)()
+        saved_load(2, low, cols(j), zb.at[j % 2], load.at[4 + j % 2], act)
+
+    def attn_loads(low, act):
+        getattr(pltpu.make_async_copy(w_out.at[n_layers - 2 - low], wo, load.at[6]), act)()
+        saved_load(1, low, None, hb, load.at[7], act)
+
+    def last_loads(low, act):
+        getattr(pltpu.make_async_copy(w_qkv.at[n_layers - 2 - low], wq, load.at[9]), act)()
+        saved_load(0, low, None, xb, load.at[10], act)
+
+    def add_gain(row, value):
+        rows = lax.broadcasted_iota(jnp.int32, gs.shape[1:], 0)
+        gs[0] = gs[0] + jnp.where(rows == row, value, 0.0)
+
+    def prologue():
+        first = pltpu.make_async_copy(dx_hbm[0], dy, load.at[11])
+        first.start()
+        mlp_loads(jnp.int32(0), jnp.int32(0), 'start')
+        first.wait()
+
+    def dz_out(low, j):
+        return pltpu.make_async_copy(dz.at[:, cols(j)], dz_hbm.at[low, :, cols(j)], store.at[j])
+
+    def piece(t):
+        low, p = (t - 1) // PIECES, (t - 1) % PIECES
+        layer = n_layers - 2 - low
+        active = (t >= 1) & (t <= n_low * PIECES)
+
+        @pl.when(active & (p < 4))
+        def _():
+            mlp_loads(low, p, 'wait')
+
+            @pl.when(p < 3)
+            def _():
+                mlp_loads(low, p + 1, 'start')
+
+            @pl.when(p == 3)
+            def _():
+                attn_loads(low, 'start')
+                saved_load(3, low, None, qkvb, load.at[8], 'start')
+
+            slot = p % 2
+            grad_act = dot_nt(dy[...], w2[slot]).astype(jnp.bfloat16).astype(jnp.float32)
+            grad_pre = (gelu_slope(zb[slot].astype(jnp.float32)) * grad_act).astype(jnp.bfloat16)
+            dz[:, cols(p)] = grad_pre
+            term = dot_nt(grad_pre, w1[slot])
+
+            @pl.when(p == 0)
+            def _():
+                acc[...] = term
+
+            @pl.when(p > 0)
+            def _():
+                acc[...] = acc[...] + term
+
+            dz_out(low, p).start()
+
+        @pl.when(active & (p == 4))
+        def _():
+            attn_loads(low, 'wait')
+            last_loads(low, 'start')
+            grad_out = acc[...].astype(jnp.bfloat16).astype(jnp.float32)
+            gain = gain_two[pl.ds(layer, 1), :]
+            grad_rows, grad_gain = norm_grad(hb[...].astype(jnp.float32), gain, grad_out)
+            dh[...] = (dy[...].astype(jnp.float32) + grad_rows).astype(jnp.bfloat16)
+            add_gain(n_layers + layer, grad_gain)
+            do[...] = dot_nt(dh[...], wo[...]).astype(jnp.bfloat16)
+            pltpu.make_async_copy(dh, dh_hbm.at[low], store.at[4]).start()
+            saved_load(3, low, None, qkvb, load.at[8], 'wait')
+            for j in range(4):
+                dz_out(low, j).wait()
+
+        @pl.when(active & (p >= 5) & (p < 11))
+        def _():
+            def pair_cols(part_idx):
+                return pl.ds(pl.multiple_of(part_idx * WIDTH + (p - 5) * 2 * HEAD_DIM, 2 * HEAD_DIM), 2 * HEAD_DIM)
+
+            pair = pair_grads(qkvb[:, pair_cols(0)], qkvb[:, pair_cols(1)], qkvb[:, pair_cols(2)], do[:, pair_cols(0)])
+            for part_idx in range(3):
+                dqkv[:, pair_cols(part_idx)] = pair[part_idx]
+
+        @pl.when(active & (p == 11))
+        def _():
+            last_loads(low, 'wait')
+            dqkv_out = pltpu.make_async_copy(dqkv, dqkv_hbm.at[low], store.at[5])
+            dqkv_out.start()
+
+            @pl.when(low + 1 < n_low)
+            def _():
+                mlp_loads(low + 1, jnp.int32(0), 'start')
+
+            grad_out = dot_nt(dqkv[...], wq[...]).astype(jnp.bfloat16).astype(jnp.float32)
+            gain = gain_one[pl.ds(layer, 1), :]
+            grad_rows, grad_gain = norm_grad(xb[...].astype(jnp.float32), gain, grad_out)
+            add_gain(layer, grad_gain)
+            dy[...] = (dh[...].astype(jnp.float32) + grad_rows).astype(jnp.bfloat16)
+            for which in range(n_low):
+                dst = grad_x if which == n_low - 1 else dx_hbm[which + 1]
+
+                @pl.when(low == which)
+                def _():
+                    out = pltpu.make_async_copy(dy, dst, store.at[6])
+                    out.start()
+                    out.wait()
+
+            pltpu.make_async_copy(dh, dh_hbm.at[low], store.at[4]).wait()
+            dqkv_out.wait()
+
+    return prologue, piece
+
+
+def reduce_kernel(n_layers, n_tile, n_dev, *refs):
+    refs = list(refs)
+
+    def take(count):
+        out = refs[:count]
+        del refs[:count]
+        return out
+
+    n_low = n_layers - 1
+    top = take(8)
+    lower = [take(4) for _ in range(n_low)]
+    saved = [take(4) for _ in range(n_low)]
+    weights = take(4)
+    gain_one, gain_two, gain_ref, dx_top = take(4)
+    g_ref, gain_out, grad_x, dqkv_hbm, dh_hbm, dz_hbm, dx_mid = take(7)
+    dx_hbm = [dx_top] + [dx_mid.at[which] for which in range(n_low - 1)]
+    gs, *vm = take(15)
+    load, store = take(2)
+    prologue, piece = backward_pieces(n_layers, saved, weights, gain_one, gain_two, (dqkv_hbm, dh_hbm, dz_hbm), dx_hbm, grad_x, gs, vm, load, store)
+    f_refs = list(top)
+    for low in range(n_low):
+        u_one, attn_out, u_two, act_lo = lower[low]
+        f_refs += [u_one, dqkv_hbm.at[low], attn_out, dh_hbm.at[low], u_two, dz_hbm.at[low], act_lo, dx_hbm[low]]
+    reduce_body(n_tile, n_dev, prologue, piece, n_low * PIECES + 2, f_refs, gain_ref, g_ref, gain_out, gs, *refs)
+
+
+def reduce_body(n_tile, n_dev, prologue, piece, gain_start, f_refs, gain_ref, g_ref, gain_out, gs, gr, gz, gs_s, gs_r, gz_s, gz_r, fa, fb, part, ra, acc, rzb, rza, rb, fin,
+                fl_a, fl_b, fs_a, fs_b, fr_a, fr_b,
+                ra_s, ra_r, z_s, zb_r, za_r, b_s, b_r, bag_s, bag_r, loc, bc_r, up_s, dn_s, aag_s, aag_r, p1_s, p1_r, p2_s, p2_r):
     toks = f_refs[0].shape[0]
     half = WIDTH // 2
     n_slot = fa.shape[0]
@@ -396,13 +572,12 @@
         return remote(gs.at[3], gz.at[slot], gz_s.at[dist], gz_r.at[slot], z_devs[dist])
 
     def gain_steps(t):
-        @pl.when(t == 0)
+        @pl.when(t == gain_start)
         def _():
-            gs[0] = gain_ref[...]
             gain_copy(0).start()
 
         for hop in range(1, 4):
-            @pl.when(t == 4 * hop)
+            @pl.when(t == gain_start + 4 * hop)
             def _():
                 gain_copy(hop - 1).wait()
                 gs[hop] = gs[hop - 1] + gr[hop - 1]
@@ -413,7 +588,7 @@
                     for dist in range(top_z):
                         gain_line(dist, my_z).start()
 
-        @pl.when(t == 16)
+        @pl.when(t == gain_start + 16)
         def _():
             for dist in range(top_z):
                 gain_line(dist, my_z).wait_send()
@@ -458,25 +633,37 @@
             for stages in streams:
                 stages[0](t)
 
+        piece(t)
         return carry
 
+    gs[0] = gain_ref[...]
+    prologue()
     lax.fori_loop(0, n_unit + HOP * (n_stage - 1), step, 0)
 
 
-def reduce_tiles(factors, gains, n_tile, n_dev):
-    toks = factors[0].shape[0]
+def reduce_tiles(top_factors, lower, saved, weights, gain_one, gain_two, gains, dx_top, n_tile, n_dev):
+    n_layers = len(lower) + 1
+    n_low = n_layers - 1
+    toks = dx_top.shape[0]
     half = WIDTH // 2
     f32, bf16 = jnp.float32, jnp.bfloat16
     dma = pltpu.SemaphoreType.DMA
     slots = pltpu.VMEM((2, RING, 2 * SUB, WIDTH), f32)
     flops = n_tile * 2 * half * 2 * toks * WIDTH
+    anyspace, vmem = pl.BlockSpec(memory_space=pl.ANY), pl.BlockSpec(memory_space=pltpu.VMEM)
+    operands = list(top_factors) + [ref for group in lower for ref in group] + [ref for group in saved for ref in group] + list(weights)
+    outs = [(((n_tile * WIDTH, WIDTH), f32), anyspace), ((gains.shape, f32), vmem), (((toks, WIDTH), bf16), anyspace),
+            (((n_low, toks, 3 * WIDTH), bf16), anyspace), (((n_low, toks, WIDTH), bf16), anyspace), (((n_low, toks, 4 * WIDTH), bf16), anyspace),
+            (((max(n_low - 1, 1), toks, WIDTH), bf16), anyspace)]
+    vm_shapes = [(2, WIDTH, WIDTH), (2, WIDTH, WIDTH), (2, toks, WIDTH), (toks, WIDTH), (WIDTH, WIDTH), (toks, 3 * WIDTH), (WIDTH, 3 * WIDTH), (toks, WIDTH),
+                 (toks, 4 * WIDTH), (toks, WIDTH), (toks, 3 * WIDTH), (toks, WIDTH), (toks, WIDTH)]
     return pl.pallas_call(
-        functools.partial(reduce_kernel, n_tile, n_dev),
-        out_shape=(jax.ShapeDtypeStruct((n_tile * WIDTH, WIDTH), f32), jax.ShapeDtypeStruct(gains.shape, f32)),
-        in_specs=[pl.BlockSpec(memory_space=pl.ANY)] * len(factors) + [pl.BlockSpec(memory_space=pltpu.VMEM)],
-        out_specs=(pl.BlockSpec(memory_space=pl.ANY), pl.BlockSpec(memory_space=pltpu.VMEM)),
-        scratch_shapes=[
-            pltpu.VMEM((4,) + gains.shape, f32),
+        functools.partial(reduce_kernel, n_layers, n_tile, n_dev),
+        out_shape=tuple(jax.ShapeDtypeStruct(*shape) for shape, _ in outs),
+        in_specs=[anyspace] * len(operands) + [vmem, vmem, vmem, anyspace],
+        out_specs=tuple(spec for _, spec in outs),
+        scratch_shapes=[pltpu.VMEM((4,) + gains.shape, f32)] + [pltpu.VMEM(shape, bf16) for shape in vm_shapes] + [
+            pltpu.VMEM((toks, WIDTH), f32), dma((12,)), dma((7,)),
             pltpu.VMEM((3,) + gains.shape, f32),
             pltpu.VMEM((n_dev // 8,) + gains.shape, f32),
             dma((3,)), dma((3,)), dma((n_dev // 8 - 1,)), dma((n_dev // 8,)),
@@ -487,10 +674,10 @@
             pltpu.VMEM((2, RING, SUB, WIDTH), f32),
             pltpu.VMEM((2, RING, SUB, WIDTH), f32),
         ] + [dma((4,))] * 6 + [dma((2, RING))] * 19,
-        compiler_params=pltpu.CompilerParams(collective_id=0, has_side_effects=True, vmem_limit_bytes=48 * 1024 * 1024),
+        compiler_params=pltpu.CompilerParams(collective_id=0, has_side_effects=True, vmem_limit_bytes=62 * 1024 * 1024),
         cost_estimate=pl.CostEstimate(flops=flops, bytes_accessed=n_tile * WIDTH * WIDTH * 8, transcendentals=0),
         name='reduce_tiles',
-    )(*factors, gains)
+    )(*operands, gain_one, gain_two, gains, dx_top)
 
 
 def spread_kernel(n_layers, src_ref, qkv_ref, out_ref, up_ref, down_ref, buf, read_sem, write_sem):
@@ -506,7 +693,7 @@
             else:
                 dst = down_ref.at[layer, pl.ds((j - 8) * WIDTH, WIDTH)]
             slot = len(moves) % SPREAD
-            moves.append((pltpu.make_async_copy(src_ref.at[pl.ds((layer * TILES + j) * WIDTH, WIDTH)], buf.at[slot], read_sem.at[slot]),
+            moves.append((pltpu.make_async_copy(src_ref.at[pl.ds(((n_layers - 1 - layer) * TILES + j) * WIDTH, WIDTH)], buf.at[slot], read_sem.at[slot]),
                           pltpu.make_async_copy(buf.at[slot], dst, write_sem.at[slot])))
     ahead = SPREAD // 2
     for read, _ in moves[:ahead]:
@@ -543,20 +730,19 @@
     def local_step(x_loc, grad_y_loc, gain_one, gain_two, w_qkv, w_out, w_up, w_down):
         n_layers = w_qkv.shape[0]
         hidden_x = x_loc[0]
-        saved_all = []
+        lower, saved = [], []
         for layer_idx in range(n_layers):
-            hidden, act_lo, saved_vals = block_forward(hidden_x, gain_one[layer_idx], gain_two[layer_idx], w_qkv[layer_idx], w_out[layer_idx], w_up[layer_idx])
-            saved_all.append(saved_vals)
+            hidden, act_lo, saved_vals, sent, kept = block_forward(hidden_x, gain_one[layer_idx], gain_two[layer_idx], w_qkv[layer_idx], w_out[layer_idx], w_up[layer_idx])
             if layer_idx + 1 < n_layers:
+                lower.insert(0, sent)
+                saved.insert(0, kept)
                 hidden_x = hidden + mix_lo('sf,fd->sd', act_lo, w_down[layer_idx])
-        grad_cur = grad_y_loc[0]
-        all_factors = [None] * n_layers
-        gain_grads = [None] * (2 * n_layers)
-        for layer_idx in reversed(range(n_layers)):
-            grad_cur, gain_grads[layer_idx], gain_grads[n_layers + layer_idx], all_factors[layer_idx] = block_backward(grad_cur, saved_all[layer_idx], w_qkv[layer_idx], w_out[layer_idx], w_up[layer_idx], w_down[layer_idx])
-        gains = jnp.stack(gain_grads + [jnp.zeros_like(gain_grads[0])] * (-2 * n_layers % 8))
-        tiles, gain_sum = reduce_tiles([factor for layer in all_factors for factor in layer], gains, n_layers * TILES, n_dev)
-        return (grad_cur[None], gain_sum[:n_layers], gain_sum[n_layers:2 * n_layers]) + tuple(spread_tiles(tiles, n_layers))
+        top = n_layers - 1
+        dx_top, top_one, top_two, factors = block_backward(grad_y_loc[0], saved_vals, w_qkv[top], w_out[top], w_up[top], w_down[top])
+        zero = jnp.zeros_like(top_one)
+        gains = jnp.stack([zero] * top + [top_one] + [zero] * top + [top_two] + [zero] * (-2 * n_layers % 8))
+        tiles, gain_sum, grad_x = reduce_tiles(factors, lower, saved, (w_qkv, w_out, w_up, w_down), gain_one, gain_two, gains, dx_top, n_layers * TILES, n_dev)[:3]
+        return (grad_x[None], gain_sum[:n_layers], gain_sum[n_layers:2 * n_layers]) + tuple(spread_tiles(tiles, n_layers))
 
     batch_spec = P('data')
     full_spec = P()

time: 814 us -> 743 us (0.913)
  matrix products: 113 us -> 73.6 us
  Pallas kernels: 671 us -> 649 us
    dot_general x23 -> x15, matrix products: 113 us -> 73.6 us  [mix_lo(): jnp.einsum(einsum_spec, lhs_arr, rhs_arr, preferred_element_type=jnp.floa...]
    pallas_call x3 -> x1, Pallas kernels: 35 us -> 11.6 us  [attention_grad(): pl.pallas_call(attn_bwd_kernel, grid=(pairs,), in_specs=specs + attn_spec...]
where the time goes in v3:
time: 743 us; the launch traced here: 734 us
  Pallas kernels  649 us (87%)
  matrix products  73.6 us (10%)
    pallas_call x1, Pallas kernels, reduce_tiles(): pl.pallas_call(functools.partial(reduce_kernel, n_layers, n_tile, n_dev),...  556 us
    dot_general x15, matrix products, mix_lo(): jnp.einsum(einsum_spec, lhs_arr, rhs_arr, preferred_element_type=jnp.floa...  73.6 us
    pallas_call x1, Pallas kernels, spread_tiles(): pl.pallas_call(functools.partial(spread_kernel, n_layers), out_shape=tupl...  56.3 us
    pallas_call x3, Pallas kernels, attention(): pl.pallas_call(attn_fwd_kernel, grid=(pairs,), in_specs=specs, out_specs=...  24.2 us

profile of v3, /device:TPU:0, one launch (start us, length us, event | category | flops | bytes accessed | tf_op | source)
XLA Modules:
  0.0 733.9 jit_solution(6975270590539806684)
XLA Ops:
  0.6 1.3 fusion.94
  1.9 0.9 slice_reduce_fusion.1
  2.8 0.8 slice_reduce_fusion
  3.6 5.0 convolution_convert_fusion.2.q_ref.k_ref.v_ref.refs_23_
  8.6 8.0 %attn_fwd.3.refs_13_ = bf16[384,768]{1,0:T(8,128)(2,1)} custom-call(bf16[384,2304]{1,0:T(8,128)(2,1)} %convolution_convert_fusion.2.q_ref.k_ref.v_ref.refs_23_, bf16[384,2304]{1,0:T(8,128)(2,1)} %convolution_convert_fusion.2.q_ref.k_ref.v_ref.refs_23_, bf16[384,2304]{1,0:T(8,128)(2,1)} %convolution_convert_fusion.2.q_ref.k_ref.v_ref.refs_23_), custom_call_target="tpu_custom_call" | custom-call | tf_op jit(solution)/shard_map/attn_fwd/pallas_call | solution.py:94
  16.7 2.2 fusion.97
  19.1 6.9 fusion.10
  26.0 6.3 fusion.100
  32.5 5.0 convolution_convert_fusion.1.q_ref.k_ref.v_ref.refs_19_
  37.5 8.2 %attn_fwd.4.refs_9_ = bf16[384,768]{1,0:T(8,128)(2,1)} custom-call(bf16[384,2304]{1,0:T(8,128)(2,1)} %convolution_convert_fusion.1.q_ref.k_ref.v_ref.refs_19_, bf16[384,2304]{1,0:T(8,128)(2,1)} %convolution_convert_fusion.1.q_ref.k_ref.v_ref.refs_19_, bf16[384,2304]{1,0:T(8,128)(2,1)} %convolution_convert_fusion.1.q_ref.k_ref.v_ref.refs_19_), custom_call_target="tpu_custom_call" | custom-call | tf_op jit(solution)/shard_map/attn_fwd/pallas_call | solution.py:94
  45.7 2.2 fusion.103
  48.1 6.9 fusion.16
  55.1 6.3 fusion.112
  61.4 1.1 fusion.93
  62.5 0.8 copy-done.13
  63.3 4.8 convolution_convert_fusion.q_ref.k_ref.v_ref
  68.1 8.0 %attn_fwd.5.refs_2_ = bf16[384,768]{1,0:T(8,128)(2,1)} custom-call(bf16[384,2304]{1,0:T(8,128)(2,1)} %convolution_convert_fusion.q_ref.k_ref.v_ref, bf16[384,2304]{1,0:T(8,128)(2,1)} %convolution_convert_fusion.q_ref.k_ref.v_ref, bf16[384,2304]{1,0:T(8,128)(2,1)} %convolution_convert_fusion.q_ref.k_ref.v_ref), custom_call_target="tpu_custom_call" | custom-call | tf_op jit(solution)/shard_map/attn_fwd/pallas_call | solution.py:94
  76.1 2.2 fusion.114
  78.3 0.2 fusion.92.refs_4_
  78.5 6.9 fusion.22
  85.5 6.3 fusion.3.refs_5_
  91.8 5.4 fusion.106
  97.3 0.4 fusion.109.refs_3_
  97.7 3.0 convolution_convert_fusion.3.do_ref
  100.7 11.6 %attn_bwd.1.refs_1_ = bf16[384,2304]{1,0:T(8,128)(2,1)} custom-call(bf16[384,2304]{1,0:T(8,128)(2,1)} %convolution_convert_fusion.q_ref.k_ref.v_ref, bf16[384,2304]{1,0:T(8,128)(2,1)} %convolution_convert_fusion.q_ref.k_ref.v_ref, bf16[384,2304]{1,0:T(8,128)(2,1)} %convolution_convert_fusion.q_ref.k_ref.v_ref, bf16[384,768]{1,0:T(8,128)(2,1)} %convolution_convert_fusion.3.do_ref), custom_call_target="tpu_custom_call" | custom-call | tf_op jit(solution)/shard_map/attn_bwd/pallas_call | solution.py:103
  112.3 4.3 fusion.113
  116.5 1.2 fusion.111.refs_31_
  117.8 0.6 stack.2.refs_30_
  118.4 556.5 %reduce_tiles.1 = (f32[27648,768]{1,0:T(8,128)}, f32[8,768]{1,0:T(8,128)}, bf16[384,768]{1,0:T(8,128)(2,1)}, bf16[2,384,2304]{2,1,0:T(8,128)(2,1)}, bf16[2,384,7...) custom-call(bf16[384,768]{1,0:T(8,128)(2,1)} %copy-done.13, ...), custom_call_target="tpu_custom_call" | custom-call | flops 16307453952 | bytes 169869312 | tf_op jit(solution)/shard_map/reduce_tiles/pallas_call | solution.py:660
  674.9 1.4 fusion.133
  676.3 56.3 %spread_tiles.1 = (f32[3,768,2304]{2,1,0:T(8,128)}, f32[3,768,768]{2,1,0:T(8,128)}, f32[3,768,3072]{2,1,0:T(8,128)}, f32[3,3072,768]{2,1,0:T(8,128)}) custom-call(f32[27648,768]{1,0:T(8,128)} %get-tuple-element.16.src_ref), custom_call_target="tpu_custom_call" | custom-call | tf_op jit(solution)/shard_map/spread_tiles/pallas_call | solution.py:716
  732.6 0.8 copy.16
  (43 shorter events, 0.7 us)
Async XLA Ops:
  8.6 8.1 %copy-start = (bf16[1,384,768]{2,1,0:T(8,128)(2,1)S(1)}, bf16[1,384,768]{2,1,0:T(8,128)(2,1)}, u32[]{:S(2)}) copy-start(bf16[1,384,768]{2,1,0:T(8,128)(2,1)} %param.8) | copy-start | bytes 1769476
  18.8 7.2 copy-start.5
  19.1 6.9 copy-start.6
  26.0 6.3 copy-start.2
  32.3 13.4 %copy-start.7 = (bf16[384,768]{1,0:T(8,128)(2,1)}, bf16[384,768]{1,0:T(8,128)(2,1)S(1)}, u32[]{:S(2)}) copy-start(bf16[384,768]{1,0:T(8,128)(2,1)S(1)} %get-tuple-element.36.refs_16_) | copy-start | bytes 1769476
  32.5 5.0 copy-start.8
  47.9 7.2 copy-start.9
  48.1 6.9 copy-start.10
  55.1 6.3 copy-start.3
  62.5 0.8 copy-start.13
  78.5 7.0 copy-start.11
  78.5 7.0 copy-start.12
  91.8 5.4 copy-start.4
  97.7 18.8 %copy-start.1 = (bf16[384,768]{1,0:T(8,128)(2,1)}, bf16[384,768]{1,0:T(8,128)(2,1)S(1)}, u32[]{:S(2)}) copy-start(bf16[384,768]{1,0:T(8,128)(2,1)S(1)} %fusion.109.refs_3_) | copy-start | bytes 1769476
  676.3 56.3 %copy-start.14 = (bf16[384,768]{1,0:T(8,128)(2,1)S(1)}, bf16[384,768]{1,0:T(8,128)(2,1)}, u32[]{:S(2)}) copy-start(bf16[384,768]{1,0:T(8,128)(2,1)} %get-tuple-element.14) | copy-start | bytes 1769476

commit v4 on v3

--- a/solution.py
+++ b/solution.py
@@ -12,11 +12,11 @@
 HEAD_DIM = 64
 WIDTH = 768
 TILES = 12
-SUB = 16
-RING = 16
+SUB = 8
+RING = 24
 SPREAD = 8
 PIECES = 12
-HOP = 2
+HOP = 3
 MESH_ID = pl.DeviceIdType.MESH
 
 
@@ -46,7 +46,7 @@
     cols = lax.broadcasted_iota(jnp.int32, scores.shape, 1)
     scores = jnp.where(rows >= cols, scores, -1e30)
     weights = jnp.exp(scores - jnp.max(scores, axis=-1, keepdims=True))
-    return weights / jnp.sum(weights, axis=-1, keepdims=True)
+    return weights * (1.0 / jnp.sum(weights, axis=-1, keepdims=True))
 
 
 def pair_masks(shape):
@@ -76,13 +76,6 @@
     return [jnp.where(first, grads[0][idx], grads[1][idx]).astype(jnp.bfloat16) for idx in range(3)]
 
 
-def attn_bwd_kernel(q_ref, k_ref, v_ref, do_ref, dqkv_ref):
-    pair = pair_grads(q_ref[...], k_ref[...], v_ref[...], do_ref[...])
-    for part_idx in range(3):
-        cols = pl.ds(pl.multiple_of(part_idx * WIDTH + pl.program_id(0) * 2 * HEAD_DIM, 2 * HEAD_DIM), 2 * HEAD_DIM)
-        dqkv_ref[:, cols] = pair[part_idx]
-
-
 def attn_specs(rows, count):
     pairs = WIDTH // (2 * HEAD_DIM)
     return pairs, [pl.BlockSpec((rows, 2 * HEAD_DIM), lambda h, lo=lo * pairs: (0, lo + h)) for lo in range(count)]
@@ -97,51 +90,21 @@
     )(qkv, qkv, qkv)
 
 
-def attention_grad(qkv, grad_attn):
-    rows = qkv.shape[0]
-    pairs, specs = attn_specs(rows, 3)
-    return pl.pallas_call(
-        attn_bwd_kernel, grid=(pairs,), in_specs=specs + attn_specs(rows, 1)[1], out_specs=pl.BlockSpec((rows, 3 * WIDTH), lambda h: (0, 0)),
-        out_shape=jax.ShapeDtypeStruct((rows, 3 * WIDTH), jnp.bfloat16), name='attn_bwd',
-    )(qkv, qkv, qkv, grad_attn)
-
-
 def block_forward(x_blk, gain_a, gain_b, w_qkv, w_out, w_up):
-    norm_a, norm_a_back = jax.vjp(rms_gain, x_blk.astype(jnp.float32), gain_a)
-    u_one = norm_a.astype(jnp.bfloat16)
+    u_one = rms_gain(x_blk.astype(jnp.float32), gain_a).astype(jnp.bfloat16)
     qkv_lo = mix_lo('sd,de->se', u_one, w_qkv)
     attn_out = attention(qkv_lo)
     hidden = x_blk + mix_lo('sd,de->se', attn_out, w_out)
-    norm_b, norm_b_back = jax.vjp(rms_gain, hidden.astype(jnp.float32), gain_b)
-    u_two = norm_b.astype(jnp.bfloat16)
+    u_two = rms_gain(hidden.astype(jnp.float32), gain_b).astype(jnp.bfloat16)
     pre_lo = mix_lo('sd,df->sf', u_two, w_up)
-    act_f, gelu_back = jax.vjp(gelu_tanh, pre_lo.astype(jnp.float32))
-    act_lo = act_f.astype(jnp.bfloat16)
-    saved_vals = (norm_a_back, u_one, qkv_lo, attn_out, norm_b_back, u_two, gelu_back, act_lo)
-    return hidden, act_lo, saved_vals, (u_one, attn_out, u_two, act_lo), (x_blk, hidden, pre_lo, qkv_lo)
-
-
-def block_backward(grad_blk, saved_vals, w_qkv, w_out, w_up, w_down):
-    (norm_a_back, u_one, qkv_lo, attn_out, norm_b_back, u_two, gelu_back, act_lo) = saved_vals
-    grad_act = mix_lo('sd,fd->sf', grad_blk, w_down)
-    (grad_pre_f,) = gelu_back(grad_act.astype(jnp.float32))
-    grad_pre = grad_pre_f.astype(jnp.bfloat16)
-    grad_u_two = mix_lo('sf,df->sd', grad_pre, w_up)
-    grad_h_norm, grad_gain_b = norm_b_back(grad_u_two.astype(jnp.float32))
-    grad_hidden = (grad_blk.astype(jnp.float32) + grad_h_norm).astype(jnp.bfloat16)
-    grad_attn = mix_lo('se,de->sd', grad_hidden, w_out)
-    grad_qkv = attention_grad(qkv_lo, grad_attn)
-    grad_u_one = mix_lo('se,de->sd', grad_qkv, w_qkv)
-    grad_x_norm, grad_gain_a = norm_a_back(grad_u_one.astype(jnp.float32))
-    grad_x_blk = (grad_hidden.astype(jnp.float32) + grad_x_norm).astype(jnp.bfloat16)
-    factors = (u_one, grad_qkv, attn_out, grad_hidden, u_two, grad_pre, act_lo, grad_blk)
-    return grad_x_blk, grad_gain_a, grad_gain_b, factors
+    act_lo = gelu_tanh(pre_lo.astype(jnp.float32)).astype(jnp.bfloat16)
+    return hidden, act_lo, (u_one, attn_out, u_two, act_lo), (x_blk, hidden, pre_lo, qkv_lo)
 
 
 def layer_tiles(factors):
     u_one, grad_qkv, attn_out, grad_hidden, u_two, grad_pre, act_lo, grad_blk = factors
     tiles = []
-    for lhs, rhs in ((u_one, grad_qkv), (attn_out, grad_hidden), (u_two, grad_pre), (act_lo, grad_blk)):
+    for lhs, rhs in ((act_lo, grad_blk), (u_two, grad_pre), (attn_out, grad_hidden), (u_one, grad_qkv)):
         tiles += [(lhs, left, rhs, right) for left in range(0, lhs.shape[1], WIDTH) for right in range(0, rhs.shape[1], WIDTH)]
     return tiles
 
@@ -160,17 +123,17 @@
     return 0.5 * (1.0 + curve) + 0.5 * z * (1.0 - curve * curve) * const * (1.0 + 3.0 * 0.044715 * (z * z))
 
 
-def backward_pieces(n_layers, saved, weights, gain_one, gain_two, grads_hbm, dx_hbm, grad_x, gs, vm, load, store):
+def backward_pieces(n_layers, stride, saved, weights, gain_one, gain_two, grads_hbm, dx_hbm, grad_x, gs, vm, load, store):
     w_qkv, w_out, w_up, w_down = weights
     dqkv_hbm, dh_hbm, dz_hbm = grads_hbm
     w2, w1, zb, hb, wo, qkvb, wq, xb, dz, dh, dqkv, dy, do, acc = vm
-    n_low = n_layers - 1
+    n_low = n_layers
 
     def cols(j):
         return pl.ds(pl.multiple_of(j * WIDTH, WIDTH), WIDTH)
 
     def weight_loads(low, j):
-        layer, slot = n_layers - 2 - low, j % 2
+        layer, slot = n_layers - 1 - low, j % 2
         return (pltpu.make_async_copy(w_down.at[layer, cols(j)], w2.at[slot], load.at[slot]),
                 pltpu.make_async_copy(w_up.at[layer, :, cols(j)], w1.at[slot], load.at[2 + slot]))
 
@@ -188,11 +151,11 @@
         saved_load(2, low, cols(j), zb.at[j % 2], load.at[4 + j % 2], act)
 
     def attn_loads(low, act):
-        getattr(pltpu.make_async_copy(w_out.at[n_layers - 2 - low], wo, load.at[6]), act)()
+        getattr(pltpu.make_async_copy(w_out.at[n_layers - 1 - low], wo, load.at[6]), act)()
         saved_load(1, low, None, hb, load.at[7], act)
 
     def last_loads(low, act):
-        getattr(pltpu.make_async_copy(w_qkv.at[n_layers - 2 - low], wq, load.at[9]), act)()
+        getattr(pltpu.make_async_copy(w_qkv.at[n_layers - 1 - low], wq, load.at[9]), act)()
         saved_load(0, low, None, xb, load.at[10], act)
 
     def add_gain(row, value):
@@ -209,9 +172,10 @@
         return pltpu.make_async_copy(dz.at[:, cols(j)], dz_hbm.at[low, :, cols(j)], store.at[j])
 
     def piece(t):
-        low, p = (t - 1) // PIECES, (t - 1) % PIECES
-        layer = n_layers - 2 - low
-        active = (t >= 1) & (t <= n_low * PIECES)
+        count = (t - 1) // stride
+        low, p = count // PIECES, count % PIECES
+        layer = n_layers - 1 - low
+        active = (t >= 1) & ((t - 1) % stride == 0) & (count < n_low * PIECES)
 
         @pl.when(active & (p < 4))
         def _():
@@ -304,25 +268,24 @@
         del refs[:count]
         return out
 
-    n_low = n_layers - 1
-    top = take(8)
-    lower = [take(4) for _ in range(n_low)]
-    saved = [take(4) for _ in range(n_low)]
+    lower = [take(4) for _ in range(n_layers)]
+    saved = [take(4) for _ in range(n_layers)]
     weights = take(4)
-    gain_one, gain_two, gain_ref, dx_top = take(4)
+    gain_one, gain_two, dx_top = take(3)
     g_ref, gain_out, grad_x, dqkv_hbm, dh_hbm, dz_hbm, dx_mid = take(7)
-    dx_hbm = [dx_top] + [dx_mid.at[which] for which in range(n_low - 1)]
+    dx_hbm = [dx_top] + [dx_mid.at[which] for which in range(n_layers - 1)]
     gs, *vm = take(15)
     load, store = take(2)
-    prologue, piece = backward_pieces(n_layers, saved, weights, gain_one, gain_two, (dqkv_hbm, dh_hbm, dz_hbm), dx_hbm, grad_x, gs, vm, load, store)
-    f_refs = list(top)
-    for low in range(n_low):
+    stride = WIDTH // (16 * SUB) // 3
+    prologue, piece = backward_pieces(n_layers, stride, saved, weights, gain_one, gain_two, (dqkv_hbm, dh_hbm, dz_hbm), dx_hbm, grad_x, gs, vm, load, store)
+    f_refs = []
+    for low in range(n_layers):
         u_one, attn_out, u_two, act_lo = lower[low]
         f_refs += [u_one, dqkv_hbm.at[low], attn_out, dh_hbm.at[low], u_two, dz_hbm.at[low], act_lo, dx_hbm[low]]
-    reduce_body(n_tile, n_dev, prologue, piece, n_low * PIECES + 2, f_refs, gain_ref, g_ref, gain_out, gs, *refs)
-
-
-def reduce_body(n_tile, n_dev, prologue, piece, gain_start, f_refs, gain_ref, g_ref, gain_out, gs, gr, gz, gs_s, gs_r, gz_s, gz_r, fa, fb, part, ra, acc, rzb, rza, rb, fin,
+    reduce_body(n_tile, n_dev, prologue, piece, n_layers * PIECES * stride + 2, f_refs, g_ref, gain_out, gs, *refs)
+
+
+def reduce_body(n_tile, n_dev, prologue, piece, gain_start, f_refs, g_ref, gain_out, gs, gr, gz, gs_s, gs_r, gz_s, gz_r, fa, fb, part, ra, acc, rzb, rza, rb, fin,
                 fl_a, fl_b, fs_a, fs_b, fr_a, fr_b,
                 ra_s, ra_r, z_s, zb_r, za_r, b_s, b_r, bag_s, bag_r, loc, bc_r, up_s, dn_s, aag_s, aag_r, p1_s, p1_r, p2_s, p2_r):
     toks = f_refs[0].shape[0]
@@ -636,14 +599,14 @@
         piece(t)
         return carry
 
-    gs[0] = gain_ref[...]
+    gs[0] = jnp.zeros(gs.shape[1:], jnp.float32)
     prologue()
     lax.fori_loop(0, n_unit + HOP * (n_stage - 1), step, 0)
 
 
-def reduce_tiles(top_factors, lower, saved, weights, gain_one, gain_two, gains, dx_top, n_tile, n_dev):
-    n_layers = len(lower) + 1
-    n_low = n_layers - 1
+def reduce_tiles(lower, saved, weights, gain_one, gain_two, dx_top, n_tile, n_dev):
+    n_layers = n_low = len(lower)
+    gains = jax.ShapeDtypeStruct((-(-2 * n_layers // 8) * 8, WIDTH), jnp.float32)
     toks = dx_top.shape[0]
     half = WIDTH // 2
     f32, bf16 = jnp.float32, jnp.bfloat16
@@ -651,16 +614,16 @@
     slots = pltpu.VMEM((2, RING, 2 * SUB, WIDTH), f32)
     flops = n_tile * 2 * half * 2 * toks * WIDTH
     anyspace, vmem = pl.BlockSpec(memory_space=pl.ANY), pl.BlockSpec(memory_space=pltpu.VMEM)
-    operands = list(top_factors) + [ref for group in lower for ref in group] + [ref for group in saved for ref in group] + list(weights)
+    operands = [ref for group in lower for ref in group] + [ref for group in saved for ref in group] + list(weights)
     outs = [(((n_tile * WIDTH, WIDTH), f32), anyspace), ((gains.shape, f32), vmem), (((toks, WIDTH), bf16), anyspace),
             (((n_low, toks, 3 * WIDTH), bf16), anyspace), (((n_low, toks, WIDTH), bf16), anyspace), (((n_low, toks, 4 * WIDTH), bf16), anyspace),
-            (((max(n_low - 1, 1), toks, WIDTH), bf16), anyspace)]
+            (((n_layers - 1, toks, WIDTH), bf16), anyspace)]
     vm_shapes = [(2, WIDTH, WIDTH), (2, WIDTH, WIDTH), (2, toks, WIDTH), (toks, WIDTH), (WIDTH, WIDTH), (toks, 3 * WIDTH), (WIDTH, 3 * WIDTH), (toks, WIDTH),
                  (toks, 4 * WIDTH), (toks, WIDTH), (toks, 3 * WIDTH), (toks, WIDTH), (toks, WIDTH)]
     return pl.pallas_call(
         functools.partial(reduce_kernel, n_layers, n_tile, n_dev),
         out_shape=tuple(jax.ShapeDtypeStruct(*shape) for shape, _ in outs),
-        in_specs=[anyspace] * len(operands) + [vmem, vmem, vmem, anyspace],
+        in_specs=[anyspace] * len(operands) + [vmem, vmem, anyspace],
         out_specs=tuple(spec for _, spec in outs),
         scratch_shapes=[pltpu.VMEM((4,) + gains.shape, f32)] + [pltpu.VMEM(shape, bf16) for shape in vm_shapes] + [
             pltpu.VMEM((toks, WIDTH), f32), dma((12,)), dma((7,)),
@@ -677,21 +640,21 @@
         compiler_params=pltpu.CompilerParams(collective_id=0, has_side_effects=True, vmem_limit_bytes=62 * 1024 * 1024),
         cost_estimate=pl.CostEstimate(flops=flops, bytes_accessed=n_tile * WIDTH * WIDTH * 8, transcendentals=0),
         name='reduce_tiles',
-    )(*operands, gain_one, gain_two, gains, dx_top)
+    )(*operands, gain_one, gain_two, dx_top)
 
 
 def spread_kernel(n_layers, src_ref, qkv_ref, out_ref, up_ref, down_ref, buf, read_sem, write_sem):
     moves = []
     for layer in range(n_layers):
         for j in range(TILES):
-            if j < 3:
-                dst = qkv_ref.at[layer, :, pl.ds(j * WIDTH, WIDTH)]
-            elif j < 4:
-                dst = out_ref.at[layer]
+            if j < 4:
+                dst = down_ref.at[layer, pl.ds(j * WIDTH, WIDTH)]
             elif j < 8:
                 dst = up_ref.at[layer, :, pl.ds((j - 4) * WIDTH, WIDTH)]
+            elif j < 9:
+                dst = out_ref.at[layer]
             else:
-                dst = down_ref.at[layer, pl.ds((j - 8) * WIDTH, WIDTH)]
+                dst = qkv_ref.at[layer, :, pl.ds((j - 9) * WIDTH, WIDTH)]
             slot = len(moves) % SPREAD
             moves.append((pltpu.make_async_copy(src_ref.at[pl.ds(((n_layers - 1 - layer) * TILES + j) * WIDTH, WIDTH)], buf.at[slot], read_sem.at[slot]),
                           pltpu.make_async_copy(buf.at[slot], dst, write_sem.at[slot])))
@@ -732,16 +695,12 @@
         hidden_x = x_loc[0]
         lower, saved = [], []
         for layer_idx in range(n_layers):
-            hidden, act_lo, saved_vals, sent, kept = block_forward(hidden_x, gain_one[layer_idx], gain_two[layer_idx], w_qkv[layer_idx], w_out[layer_idx], w_up[layer_idx])
+            hidden, act_lo, sent, kept = block_forward(hidden_x, gain_one[layer_idx], gain_two[layer_idx], w_qkv[layer_idx], w_out[layer_idx], w_up[layer_idx])
+            lower.insert(0, sent)
+            saved.insert(0, kept)
             if layer_idx + 1 < n_layers:
-                lower.insert(0, sent)
-                saved.insert(0, kept)
                 hidden_x = hidden + mix_lo('sf,fd->sd', act_lo, w_down[layer_idx])
-        top = n_layers - 1
-        dx_top, top_one, top_two, factors = block_backward(grad_y_loc[0], saved_vals, w_qkv[top], w_out[top], w_up[top], w_down[top])
-        zero = jnp.zeros_like(top_one)
-        gains = jnp.stack([zero] * top + [top_one] + [zero] * top + [top_two] + [zero] * (-2 * n_layers % 8))
-        tiles, gain_sum, grad_x = reduce_tiles(factors, lower, saved, (w_qkv, w_out, w_up, w_down), gain_one, gain_two, gains, dx_top, n_layers * TILES, n_dev)[:3]
+        tiles, gain_sum, grad_x = reduce_tiles(lower, saved, (w_qkv, w_out, w_up, w_down), gain_one, gain_two, grad_y_loc[0], n_layers * TILES, n_dev)[:3]
         return (grad_x[None], gain_sum[:n_layers], gain_sum[n_layers:2 * n_layers]) + tuple(spread_tiles(tiles, n_layers))
 
     batch_spec = P('data')

time: 743 us -> 706 us (0.950); the launches traced: 734 us -> 704 us
  matrix products: 73.6 us -> 54.8 us
  Pallas kernels: 649 us -> 638 us
    dot_general x15 -> x11, matrix products: 73.6 us -> 54.8 us  [mix_lo(): jnp.einsum(einsum_spec, lhs_arr, rhs_arr, preferred_element_type=jnp.floa...]
    pallas_call x1 -> x0, Pallas kernels: 11.6 us -> none  [attention_grad(): pl.pallas_call(attn_bwd_kernel, grid=(pairs,), in_specs=specs + attn_spec...]
where the time goes in v4:
time: 706 us; the launch traced here: 704 us
  Pallas kernels  638 us (90%)
  matrix products  54.8 us (8%)
  local copies, waits for them, and re-layouts  7.26 us (1%)
    pallas_call x1, Pallas kernels, reduce_tiles(): pl.pallas_call(functools.partial(reduce_kernel, n_layers, n_tile, n_dev),...  558 us
    pallas_call x1, Pallas kernels, spread_tiles(): pl.pallas_call(functools.partial(spread_kernel, n_layers), out_shape=tupl...  56.3 us
    dot_general x11, matrix products, mix_lo(): jnp.einsum(einsum_spec, lhs_arr, rhs_arr, preferred_element_type=jnp.floa...  54.8 us
    pallas_call x3, Pallas kernels, attention(): pl.pallas_call(attn_fwd_kernel, grid=(pairs,), in_specs=specs, out_specs=...  24.2 us

profile of v4, /device:TPU:0, one launch (start us, length us, event | category | flops | bytes accessed | tf_op | source)
XLA Modules:
  0.0 704.4 jit_solution(13111090812792977159)
XLA Ops:
  0.6 1.3 fusion.63
  1.9 0.9 slice_reduce_fusion.1
  2.8 0.8 slice_reduce_fusion
  3.6 5.0 convolution_convert_fusion.2.q_ref.k_ref.v_ref.refs_23_
  8.6 8.0 %attn_fwd.3.refs_9_ = bf16[384,768]{1,0:T(8,128)(2,1)} custom-call(bf16[384,2304]{1,0:T(8,128)(2,1)} %convolution_convert_fusion.2.q_ref.k_ref.v_ref.refs_23_, bf16[384,2304]{1,0:T(8,128)(2,1)} %convolution_convert_fusion.2.q_ref.k_ref.v_ref.refs_23_, bf16[384,2304]{1,0:T(8,128)(2,1)} %convolution_convert_fusion.2.q_ref.k_ref.v_ref.refs_23_), custom_call_target="tpu_custom_call" | custom-call | tf_op jit(solution)/shard_map/attn_fwd/pallas_call | solution.py:87
  16.7 2.2 fusion.66
  18.9 0.2 fusion.68.refs_10_
  19.1 7.0 fusion.5
  26.1 0.0 copy-done.4
  26.1 6.3 fusion.69
  32.3 0.0 copy-start.12
  32.4 1.1 fusion.65
  33.5 0.8 copy-done.13
  34.3 4.8 convolution_convert_fusion.1.q_ref.k_ref.v_ref.refs_19_
  39.1 8.2 %attn_fwd.4.refs_5_ = bf16[384,768]{1,0:T(8,128)(2,1)} custom-call(bf16[384,2304]{1,0:T(8,128)(2,1)} %convolution_convert_fusion.1.q_ref.k_ref.v_ref.refs_19_, bf16[384,2304]{1,0:T(8,128)(2,1)} %convolution_convert_fusion.1.q_ref.k_ref.v_ref.refs_19_, bf16[384,2304]{1,0:T(8,128)(2,1)} %convolution_convert_fusion.1.q_ref.k_ref.v_ref.refs_19_), custom_call_target="tpu_custom_call" | custom-call | tf_op jit(solution)/shard_map/attn_fwd/pallas_call | solution.py:87
  47.3 2.0 fusion.72
  49.3 0.2 fusion.74.refs_6_
  49.5 6.9 fusion.11
  56.4 6.3 fusion.75
  62.7 0.8 copy-done.8
  63.5 0.2 fusion.77.refs_0_
  63.8 0.8 copy-done.9
  64.6 4.8 convolution_convert_fusion.q_ref.k_ref.v_ref.refs_15_
  69.3 8.0 %attn_fwd.5.refs_1_ = bf16[384,768]{1,0:T(8,128)(2,1)} custom-call(bf16[384,2304]{1,0:T(8,128)(2,1)} %convolution_convert_fusion.q_ref.k_ref.v_ref.refs_15_, bf16[384,2304]{1,0:T(8,128)(2,1)} %convolution_convert_fusion.q_ref.k_ref.v_ref.refs_15_, bf16[384,2304]{1,0:T(8,128)(2,1)} %convolution_convert_fusion.q_ref.k_ref.v_ref.refs_15_), custom_call_target="tpu_custom_call" | custom-call | tf_op jit(solution)/shard_map/attn_fwd/pallas_call | solution.py:87
  77.3 2.0 fusion.78
  79.3 0.8 copy-done.10
  80.1 0.2 fusion.80.refs_2_
  80.3 7.7 %fusion.17 = (bf16[384,3072]{1,0:T(8,128)(2,1)}, bf16[384,3072]{1,0:T(8,128)(2,1)}) fusion(bf16[384,768]{1,0:T(8,128)(2,1)S(1)} %fusion.80.refs_2_, bf16[3,768,3072]{2,1,0:T(8,128)(2,1)} %refs_26_.1), kind=kOutput, calls=%fused_computation.29 | convolution fusion | flops 1824915456 | bytes 10027008 | tf_op jit(solution)/shard_map/sd,df->sf/dot_general | solution.py:32
  88.0 557.8 %reduce_tiles.1 = (f32[27648,768]{1,0:T(8,128)}, f32[8,768]{1,0:T(8,128)}, bf16[384,768]{1,0:T(8,128)(2,1)}, bf16[3,384,2304]{2,1,0:T(8,128)(2,1)}, bf16[3,384,7...) custom-call(bf16[384,768]{1,0:T(8,128)(2,1)} %copy-done.9, ...), custom_call_target="tpu_custom_call" | custom-call | flops 16307453952 | bytes 169869312 | tf_op jit(solution)/shard_map/reduce_tiles/pallas_call | solution.py:623
  645.8 1.4 fusion.93
  647.3 56.3 %spread_tiles.1 = (f32[3,768,2304]{2,1,0:T(8,128)}, f32[3,768,768]{2,1,0:T(8,128)}, f32[3,768,3072]{2,1,0:T(8,128)}, f32[3,3072,768]{2,1,0:T(8,128)}) custom-call(f32[27648,768]{1,0:T(8,128)} %get-tuple-element.16.src_ref), custom_call_target="tpu_custom_call" | custom-call | tf_op jit(solution)/shard_map/spread_tiles/pallas_call | solution.py:679
  703.6 0.8 copy.16
  (30 shorter events, 0.1 us)
Async XLA Ops:
  8.6 8.1 %copy-start = (bf16[1,384,768]{2,1,0:T(8,128)(2,1)S(1)}, bf16[1,384,768]{2,1,0:T(8,128)(2,1)}, u32[]{:S(2)}) copy-start(bf16[1,384,768]{2,1,0:T(8,128)(2,1)} %param.8) | copy-start | bytes 1769476
  18.9 7.2 %copy-start.4 = (bf16[384,768]{1,0:T(8,128)(2,1)}, bf16[384,768]{1,0:T(8,128)(2,1)S(1)}, u32[]{:S(2)}) copy-start(bf16[384,768]{1,0:T(8,128)(2,1)S(1)} %get-tuple-element.30.refs_21_) | copy-start | bytes 1769476
  19.1 7.0 copy-start.5
  26.1 6.3 copy-start.2
  32.3 1.1 copy-start.12
  33.5 0.8 copy-start.13
  39.1 8.2 %copy-start.1 = (bf16[3,768,768]{2,1,0:T(8,128)(2,1)S(1)}, bf16[3,768,768]{2,1,0:T(8,128)(2,1)}, u32[]{:S(2)}) copy-start(bf16[3,768,768]{2,1,0:T(8,128)(2,1)} %refs_25_.1) | copy-start | bytes 10616836
  49.2 7.2 %copy-start.6 = (bf16[384,768]{1,0:T(8,128)(2,1)}, bf16[384,768]{1,0:T(8,128)(2,1)S(1)}, u32[]{:S(2)}) copy-start(bf16[384,768]{1,0:T(8,128)(2,1)S(1)} %get-tuple-element.34.refs_17_) | copy-start | bytes 1769476
  49.5 7.0 copy-start.7
  56.4 6.3 copy-start.3
  62.7 0.8 copy-start.8
  63.7 0.8 copy-start.9
  79.3 0.8 copy-start.10
  80.3 7.7 %copy-start.11 = (bf16[384,768]{1,0:T(8,128)(2,1)}, bf16[384,768]{1,0:T(8,128)(2,1)S(1)}, u32[]{:S(2)}) copy-start(bf16[384,768]{1,0:T(8,128)(2,1)S(1)} %fusion.80.refs_2_) | copy-start | bytes 1769476
  647.3 56.3 %copy-start.14 = (bf16[384,768]{1,0:T(8,128)(2,1)S(1)}, bf16[384,768]{1,0:T(8,128)(2,1)}, u32[]{:S(2)}) copy-start(bf16[384,768]{1,0:T(8,128)(2,1)} %get-tuple-element.14) | copy-start | bytes 1769476

commit v5 on v4

--- a/solution.py
+++ b/solution.py
@@ -13,10 +13,10 @@
 WIDTH = 768
 TILES = 12
 SUB = 8
-RING = 24
+RING = 16
 SPREAD = 8
 PIECES = 12
-HOP = 3
+HOP = 2
 MESH_ID = pl.DeviceIdType.MESH
 
 
@@ -26,10 +26,6 @@
 
 def gelu_tanh(pre_act):
     return jax.nn.gelu(pre_act, approximate=True)
-
-
-def mix_lo(einsum_spec, lhs_arr, rhs_arr):
-    return jnp.einsum(einsum_spec, lhs_arr, rhs_arr, preferred_element_type=jnp.float32).astype(jnp.bfloat16)
 
 
 def dot_nt(lhs, rhs):
@@ -52,13 +48,6 @@
 def pair_masks(shape):
     first = lax.broadcasted_iota(jnp.int32, shape, 1) < HEAD_DIM
     return first, [jnp.where(first, 1.0, 0.0).astype(jnp.bfloat16), jnp.where(first, 0.0, 1.0).astype(jnp.bfloat16)]
-
-
-def attn_fwd_kernel(q_ref, k_ref, v_ref, o_ref):
-    q_pair, k_pair, v_pair = q_ref[...], k_ref[...], v_ref[...]
-    first, masks = pair_masks(q_pair.shape)
-    outs = [jnp.dot(head_probs(q_pair * mask, k_pair).astype(jnp.bfloat16), v_pair, preferred_element_type=jnp.float32) for mask in masks]
-    o_ref[...] = jnp.where(first, outs[0], outs[1]).astype(jnp.bfloat16)
 
 
 def pair_grads(q_pair, k_pair, v_pair, do_pair):
@@ -76,29 +65,128 @@
     return [jnp.where(first, grads[0][idx], grads[1][idx]).astype(jnp.bfloat16) for idx in range(3)]
 
 
-def attn_specs(rows, count):
-    pairs = WIDTH // (2 * HEAD_DIM)
-    return pairs, [pl.BlockSpec((rows, 2 * HEAD_DIM), lambda h, lo=lo * pairs: (0, lo + h)) for lo in range(count)]
-
-
-def attention(qkv):
-    rows = qkv.shape[0]
-    pairs, specs = attn_specs(rows, 3)
+def causal_rows(q_part, k_pair, v_pair, lo, count):
+    keys = lo + count
+    scores = dot_nt(q_part[lo:keys], k_pair[:keys]) * HEAD_DIM ** -0.5
+    rows = lax.broadcasted_iota(jnp.int32, scores.shape, 0) + lo
+    cols = lax.broadcasted_iota(jnp.int32, scores.shape, 1)
+    scores = jnp.where(rows >= cols, scores, -1e30)
+    weights = jnp.exp(scores - jnp.max(scores, axis=-1, keepdims=True))
+    probs = (weights * (1.0 / jnp.sum(weights, axis=-1, keepdims=True))).astype(jnp.bfloat16)
+    return jnp.dot(probs, v_pair[:keys], preferred_element_type=jnp.float32)
+
+
+def forward_kernel(n_layers, x_ref, gain_one, gain_two, w_qkv, w_out, w_up, w_down,
+                   x_all, u_one_all, qkv_all, attn_all, hidden_all, u_two_all, z_all, act_all,
+                   wq, wo, w1, w2, x_v, u_one, qkv, attn, hidden, u_two, z_v, act, acc, load, store):
+    f32, bf16 = jnp.float32, jnp.bfloat16
+    toks = x_ref.shape[0]
+
+    def loads(layer):
+        slot = layer % 2
+        return [pltpu.make_async_copy(src.at[layer], dst.at[slot], load.at[slot, idx])
+                for idx, (src, dst) in enumerate(((w_qkv, wq), (w_out, wo), (w_up, w1), (w_down, w2)))]
+
+    def saves(layer):
+        pairs = ((x_v, x_all), (u_one, u_one_all), (qkv, qkv_all), (attn, attn_all), (hidden, hidden_all), (u_two, u_two_all), (z_v, z_all), (act, act_all))
+        return [pltpu.make_async_copy(src, dst.at[layer], store.at[idx]) for idx, (src, dst) in enumerate(pairs)]
+
+    for copy in loads(jnp.int32(0)):
+        copy.start()
+    x_v[...] = x_ref[...]
+
+    def layer_step(layer, carry):
+        slot = layer % 2
+        weights, outs = loads(layer), saves(layer)
+
+        def reuse(idx):
+            @pl.when(layer > 0)
+            def _():
+                outs[idx].wait()
+
+        @pl.when(layer + 1 < n_layers)
+        def _():
+            for copy in loads(layer + 1):
+                copy.start()
+
+        outs[0].start()
+        reuse(1)
+        u_one[...] = rms_gain(x_v[...].astype(f32), gain_one[pl.ds(layer, 1), :]).astype(bf16)
+        outs[1].start()
+        weights[0].wait()
+        reuse(2)
+        for j in range(3):
+            cols = slice(j * WIDTH, (j + 1) * WIDTH)
+            qkv[:, cols] = jnp.dot(u_one[...], wq[slot, :, cols], preferred_element_type=f32).astype(bf16)
+        outs[2].start()
+        reuse(3)
+
+        def pair_step(pair, inner):
+            def pair_cols(part_idx):
+                return pl.ds(pl.multiple_of(part_idx * WIDTH + pair * 2 * HEAD_DIM, 2 * HEAD_DIM), 2 * HEAD_DIM)
+
+            q_pair, k_pair, v_pair = (qkv[:, pair_cols(part_idx)] for part_idx in range(3))
+            first, masks = pair_masks(q_pair.shape)
+            heads = [q_pair * mask for mask in masks]
+            for lo in range(0, toks, 128):
+                out = [causal_rows(head, k_pair, v_pair, lo, 128) for head in heads]
+                attn[lo:lo + 128, pair_cols(0)] = jnp.where(first[:128], out[0], out[1]).astype(bf16)
+            return inner
+
+        lax.fori_loop(0, WIDTH // (2 * HEAD_DIM), pair_step, 0)
+        outs[3].start()
+        weights[1].wait()
+        mixed = jnp.dot(attn[...], wo[slot], preferred_element_type=f32).astype(bf16)
+        reuse(4)
+        hidden[...] = (x_v[...].astype(f32) + mixed.astype(f32)).astype(bf16)
+        outs[4].start()
+        reuse(5)
+        u_two[...] = rms_gain(hidden[...].astype(f32), gain_two[pl.ds(layer, 1), :]).astype(bf16)
+        outs[5].start()
+        weights[2].wait()
+        weights[3].wait()
+        reuse(6)
+        reuse(7)
+        for j in range(4):
+            cols = slice(j * WIDTH, (j + 1) * WIDTH)
+            pre = jnp.dot(u_two[...], w1[slot, :, cols], preferred_element_type=f32).astype(bf16)
+            z_v[:, cols] = pre
+            act[:, cols] = gelu_tanh(pre.astype(f32)).astype(bf16)
+
+            @pl.when(layer + 1 < n_layers)
+            def _():
+                term = jnp.dot(act[:, cols], w2[slot, cols], preferred_element_type=f32)
+                acc[...] = term if j == 0 else acc[...] + term
+        outs[6].start()
+        outs[7].start()
+        outs[0].wait()
+
+        @pl.when(layer + 1 < n_layers)
+        def _():
+            x_v[...] = (hidden[...].astype(f32) + acc[...].astype(bf16).astype(f32)).astype(bf16)
+
+        return carry
+
+    lax.fori_loop(0, n_layers, layer_step, 0)
+    for copy in saves(n_layers - 1)[1:]:
+        copy.wait()
+
+
+def forward(x_loc, gain_one, gain_two, weights):
+    n_layers, toks = gain_one.shape[0], x_loc.shape[0]
+    f32, bf16 = jnp.float32, jnp.bfloat16
+    anyspace, vmem = pl.BlockSpec(memory_space=pl.ANY), pl.BlockSpec(memory_space=pltpu.VMEM)
+    widths = (WIDTH, WIDTH, 3 * WIDTH, WIDTH, WIDTH, WIDTH, 4 * WIDTH, 4 * WIDTH)
     return pl.pallas_call(
-        attn_fwd_kernel, grid=(pairs,), in_specs=specs, out_specs=attn_specs(rows, 1)[1][0],
-        out_shape=jax.ShapeDtypeStruct((rows, WIDTH), jnp.bfloat16), name='attn_fwd',
-    )(qkv, qkv, qkv)
-
-
-def block_forward(x_blk, gain_a, gain_b, w_qkv, w_out, w_up):
-    u_one = rms_gain(x_blk.astype(jnp.float32), gain_a).astype(jnp.bfloat16)
-    qkv_lo = mix_lo('sd,de->se', u_one, w_qkv)
-    attn_out = attention(qkv_lo)
-    hidden = x_blk + mix_lo('sd,de->se', attn_out, w_out)
-    u_two = rms_gain(hidden.astype(jnp.float32), gain_b).astype(jnp.bfloat16)
-    pre_lo = mix_lo('sd,df->sf', u_two, w_up)
-    act_lo = gelu_tanh(pre_lo.astype(jnp.float32)).astype(jnp.bfloat16)
-    return hidden, act_lo, (u_one, attn_out, u_two, act_lo), (x_blk, hidden, pre_lo, qkv_lo)
+        functools.partial(forward_kernel, n_layers),
+        out_shape=tuple(jax.ShapeDtypeStruct((n_layers, toks, width), bf16) for width in widths),
+        in_specs=[vmem, vmem, vmem] + [anyspace] * 4,
+        out_specs=(anyspace,) * 8,
+        scratch_shapes=[pltpu.VMEM((2,) + weight.shape[1:], bf16) for weight in weights] + [pltpu.VMEM((toks, width), bf16) for width in widths] + [
+            pltpu.VMEM((toks, WIDTH), f32), pltpu.SemaphoreType.DMA((2, 4)), pltpu.SemaphoreType.DMA((8,))],
+        compiler_params=pltpu.CompilerParams(vmem_limit_bytes=58 * 1024 * 1024),
+        name='forward',
+    )(x_loc, gain_one, gain_two, *weights)
 
 
 def layer_tiles(factors):
@@ -138,12 +226,9 @@
                 pltpu.make_async_copy(w_up.at[layer, :, cols(j)], w1.at[slot], load.at[2 + slot]))
 
     def saved_load(kind, low, src_cols, dst, sem, act):
-        for which in range(n_low):
-            src = saved[which][kind] if src_cols is None else saved[which][kind].at[:, src_cols]
-
-            @pl.when(low == which)
-            def _():
-                getattr(pltpu.make_async_copy(src, dst, sem), act)()
+        layer = n_layers - 1 - low
+        src = saved[kind].at[layer] if src_cols is None else saved[kind].at[layer, :, src_cols]
+        getattr(pltpu.make_async_copy(src, dst, sem), act)()
 
     def mlp_loads(low, j, act):
         for copy in weight_loads(low, j):
@@ -268,8 +353,8 @@
         del refs[:count]
         return out
 
-    lower = [take(4) for _ in range(n_layers)]
-    saved = [take(4) for _ in range(n_layers)]
+    x_all, u_one_all, qkv_all, attn_all, hidden_all, u_two_all, z_all, act_all = take(8)
+    saved = (x_all, hidden_all, z_all, qkv_all)
     weights = take(4)
     gain_one, gain_two, dx_top = take(3)
     g_ref, gain_out, grad_x, dqkv_hbm, dh_hbm, dz_hbm, dx_mid = take(7)
@@ -280,7 +365,7 @@
     prologue, piece = backward_pieces(n_layers, stride, saved, weights, gain_one, gain_two, (dqkv_hbm, dh_hbm, dz_hbm), dx_hbm, grad_x, gs, vm, load, store)
     f_refs = []
     for low in range(n_layers):
-        u_one, attn_out, u_two, act_lo = lower[low]
+        u_one, attn_out, u_two, act_lo = (ref.at[n_layers - 1 - low] for ref in (u_one_all, attn_all, u_two_all, act_all))
         f_refs += [u_one, dqkv_hbm.at[low], attn_out, dh_hbm.at[low], u_two, dz_hbm.at[low], act_lo, dx_hbm[low]]
     reduce_body(n_tile, n_dev, prologue, piece, n_layers * PIECES * stride + 2, f_refs, g_ref, gain_out, gs, *refs)
 
@@ -604,8 +689,8 @@
     lax.fori_loop(0, n_unit + HOP * (n_stage - 1), step, 0)
 
 
-def reduce_tiles(lower, saved, weights, gain_one, gain_two, dx_top, n_tile, n_dev):
-    n_layers = n_low = len(lower)
+def reduce_tiles(saved, weights, gain_one, gain_two, dx_top, n_tile, n_dev):
+    n_layers = n_low = gain_one.shape[0]
     gains = jax.ShapeDtypeStruct((-(-2 * n_layers // 8) * 8, WIDTH), jnp.float32)
     toks = dx_top.shape[0]
     half = WIDTH // 2
@@ -614,7 +699,7 @@
     slots = pltpu.VMEM((2, RING, 2 * SUB, WIDTH), f32)
     flops = n_tile * 2 * half * 2 * toks * WIDTH
     anyspace, vmem = pl.BlockSpec(memory_space=pl.ANY), pl.BlockSpec(memory_space=pltpu.VMEM)
-    operands = [ref for group in lower for ref in group] + [ref for group in saved for ref in group] + list(weights)
+    operands = list(saved) + list(weights)
     outs = [(((n_tile * WIDTH, WIDTH), f32), anyspace), ((gains.shape, f32), vmem), (((toks, WIDTH), bf16), anyspace),
             (((n_low, toks, 3 * WIDTH), bf16), anyspace), (((n_low, toks, WIDTH), bf16), anyspace), (((n_low, toks, 4 * WIDTH), bf16), anyspace),
             (((n_layers - 1, toks, WIDTH), bf16), anyspace)]
@@ -692,15 +777,9 @@
 
     def local_step(x_loc, grad_y_loc, gain_one, gain_two, w_qkv, w_out, w_up, w_down):
         n_layers = w_qkv.shape[0]
-        hidden_x = x_loc[0]
-        lower, saved = [], []
-        for layer_idx in range(n_layers):
-            hidden, act_lo, sent, kept = block_forward(hidden_x, gain_one[layer_idx], gain_two[layer_idx], w_qkv[layer_idx], w_out[layer_idx], w_up[layer_idx])
-            lower.insert(0, sent)
-            saved.insert(0, kept)
-            if layer_idx + 1 < n_layers:
-                hidden_x = hidden + mix_lo('sf,fd->sd', act_lo, w_down[layer_idx])
-        tiles, gain_sum, grad_x = reduce_tiles(lower, saved, (w_qkv, w_out, w_up, w_down), gain_one, gain_two, grad_y_loc[0], n_layers * TILES, n_dev)[:3]
+        weights = (w_qkv, w_out, w_up, w_down)
+        saved = forward(x_loc[0], gain_one, gain_two, weights)
+        tiles, gain_sum, grad_x = reduce_tiles(saved, weights, gain_one, gain_two, grad_y_loc[0], n_layers * TILES, n_dev)[:3]
         return (grad_x[None], gain_sum[:n_layers], gain_sum[n_layers:2 * n_layers]) + tuple(spread_tiles(tiles, n_layers))
 
     batch_spec = P('data')

time: 706 us -> 684 us (0.969)
  matrix products: 54.8 us -> 0 us
  Pallas kernels: 638 us -> 680 us
    dot_general x11 -> x0, matrix products: 54.8 us -> none  [mix_lo(): jnp.einsum(einsum_spec, lhs_arr, rhs_arr, preferred_element_type=jnp.floa...]
    pallas_call x3 -> x1, Pallas kernels: 24.2 us -> 68.7 us  [forward(): pl.pallas_call(functools.partial(forward_kernel, n_layers), out_shape=tup...]
where the time goes in v5:
time: 684 us; the launch traced here: 683 us
  Pallas kernels  680 us (99%)
    pallas_call x1, Pallas kernels, reduce_tiles(): pl.pallas_call(functools.partial(reduce_kernel, n_layers, n_tile, n_dev),...  555 us
    pallas_call x1, Pallas kernels, forward(): pl.pallas_call(functools.partial(forward_kernel, n_layers), out_shape=tup...  68.7 us
    pallas_call x1, Pallas kernels, spread_tiles(): pl.pallas_call(functools.partial(spread_kernel, n_layers), out_shape=tupl...  56.3 us

profile of v5, /device:TPU:0, one launch (start us, length us, event | category | flops | bytes accessed | tf_op | source)
XLA Modules:
  0.0 683.3 jit_solution(17620925300202929231)
XLA Ops:
  0.6 68.7 %forward.1 = (bf16[3,384,768]{2,1,0:T(8,128)(2,1)}, bf16[3,384,768]{2,1,0:T(8,128)(2,1)}, bf16[3,384,2304]{2,1,0:T(8,128)(2,1)}, bf16[3,384,768]{2,1,0:T(8,128)(...) custom-call(bf16[384,768]{1,0:T(8,128)(2,1)} %bitcast.4, ...), custom_call_target="tpu_custom_call" | custom-call | tf_op jit(solution)/shard_map/forward/pallas_call | solution.py:180
  69.4 555.4 %reduce_tiles.1 = (f32[27648,768]{1,0:T(8,128)}, f32[8,768]{1,0:T(8,128)}, bf16[384,768]{1,0:T(8,128)(2,1)}, bf16[3,384,2304]{2,1,0:T(8,128)(2,1)}, bf16[3,384,7...) custom-call(bf16[3,384,768]{2,1,0:T(8,128)(2,1)} %get-tuple-element.22.refs_0_, ...), custom_call_target="tpu_custom_call" | custom-call | flops 16307453952 | bytes 169869312 | tf_op jit(solution)/shard_map/reduce_tiles/pallas_call | solution.py:708
  624.8 1.4 fusion
  626.2 0.0 copy-start
  626.2 56.3 %spread_tiles.1 = (f32[3,768,2304]{2,1,0:T(8,128)}, f32[3,768,768]{2,1,0:T(8,128)}, f32[3,768,3072]{2,1,0:T(8,128)}, f32[3,3072,768]{2,1,0:T(8,128)}) custom-call(f32[27648,768]{1,0:T(8,128)} %get-tuple-element.32.src_ref), custom_call_target="tpu_custom_call" | custom-call | tf_op jit(solution)/shard_map/spread_tiles/pallas_call | solution.py:764
  682.5 0.0 copy-done
  682.5 0.8 copy.16
Async XLA Ops:
  626.2 56.3 %copy-start = (bf16[384,768]{1,0:T(8,128)(2,1)S(1)}, bf16[384,768]{1,0:T(8,128)(2,1)}, u32[]{:S(2)}) copy-start(bf16[384,768]{1,0:T(8,128)(2,1)} %get-tuple-element.30) | copy-start | bytes 1769476

commit v6 on v5

--- a/solution.py
+++ b/solution.py
@@ -91,7 +91,7 @@
         pairs = ((x_v, x_all), (u_one, u_one_all), (qkv, qkv_all), (attn, attn_all), (hidden, hidden_all), (u_two, u_two_all), (z_v, z_all), (act, act_all))
         return [pltpu.make_async_copy(src, dst.at[layer], store.at[idx]) for idx, (src, dst) in enumerate(pairs)]
 
-    for copy in loads(jnp.int32(0)):
+    for copy in loads(jnp.int32(0))[:2]:
         copy.start()
     x_v[...] = x_ref[...]
 
@@ -103,23 +103,30 @@
             @pl.when(layer > 0)
             def _():
                 outs[idx].wait()
-
-        @pl.when(layer + 1 < n_layers)
-        def _():
-            for copy in loads(layer + 1):
-                copy.start()
 
         outs[0].start()
         reuse(1)
         u_one[...] = rms_gain(x_v[...].astype(f32), gain_one[pl.ds(layer, 1), :]).astype(bf16)
         outs[1].start()
         weights[0].wait()
+
+        @pl.when(layer == 0)
+        def _():
+            weights[2].start()
+            weights[3].start()
+
         reuse(2)
         for j in range(3):
             cols = slice(j * WIDTH, (j + 1) * WIDTH)
             qkv[:, cols] = jnp.dot(u_one[...], wq[slot, :, cols], preferred_element_type=f32).astype(bf16)
         outs[2].start()
         reuse(3)
+
+        @pl.when(layer + 1 < n_layers)
+        def _():
+            for copy in loads(layer + 1):
+                copy.start()
+
 
         def pair_step(pair, inner):
             def pair_cols(part_idx):
@@ -257,10 +264,12 @@
         return pltpu.make_async_copy(dz.at[:, cols(j)], dz_hbm.at[low, :, cols(j)], store.at[j])
 
     def piece(t):
-        count = (t - 1) // stride
+        slow = t - 1 - PIECES * stride
+        count = jnp.where(slow < 0, (t - 1) // stride, PIECES + slow // (2 * stride))
+        due = jnp.where(slow < 0, (t - 1) % stride, slow % (2 * stride)) == 0
         low, p = count // PIECES, count % PIECES
         layer = n_layers - 1 - low
-        active = (t >= 1) & ((t - 1) % stride == 0) & (count < n_low * PIECES)
+        active = (t >= 1) & due & (count < n_low * PIECES)
 
         @pl.when(active & (p < 4))
         def _():
@@ -367,7 +376,7 @@
     for low in range(n_layers):
         u_one, attn_out, u_two, act_lo = (ref.at[n_layers - 1 - low] for ref in (u_one_all, attn_all, u_two_all, act_all))
         f_refs += [u_one, dqkv_hbm.at[low], attn_out, dh_hbm.at[low], u_two, dz_hbm.at[low], act_lo, dx_hbm[low]]
-    reduce_body(n_tile, n_dev, prologue, piece, n_layers * PIECES * stride + 2, f_refs, g_ref, gain_out, gs, *refs)
+    reduce_body(n_tile, n_dev, prologue, piece, (2 * n_layers - 1) * PIECES * stride + 2, f_refs, g_ref, gain_out, gs, *refs)
 
 
 def reduce_body(n_tile, n_dev, prologue, piece, gain_start, f_refs, g_ref, gain_out, gs, gr, gz, gs_s, gs_r, gz_s, gz_r, fa, fb, part, ra, acc, rzb, rza, rb, fin,

time: 684 us -> 685 us (level)
  no operation moved by 1% of the time
where the time goes in v6:
time: 685 us
  Pallas kernels  682 us (100%)
    pallas_call x1, Pallas kernels, reduce_tiles(): pl.pallas_call(functools.partial(reduce_kernel, n_layers, n_tile, n_dev),...  557 us
    pallas_call x1, Pallas kernels, forward(): pl.pallas_call(functools.partial(forward_kernel, n_layers), out_shape=tup...  68.8 us
    pallas_call x1, Pallas kernels, spread_tiles(): pl.pallas_call(functools.partial(spread_kernel, n_layers), out_shape=tupl...  56.3 us

profile of v6, /device:TPU:0, one launch (start us, length us, event | category | flops | bytes accessed | tf_op | source)
XLA Modules:
  0.0 684.8 jit_solution(5337742290263212029)
XLA Ops:
  0.6 68.8 %forward.1 = (bf16[3,384,768]{2,1,0:T(8,128)(2,1)}, bf16[3,384,768]{2,1,0:T(8,128)(2,1)}, bf16[3,384,2304]{2,1,0:T(8,128)(2,1)}, bf16[3,384,768]{2,1,0:T(8,128)(...) custom-call(bf16[384,768]{1,0:T(8,128)(2,1)} %bitcast.4, ...), custom_call_target="tpu_custom_call" | custom-call | tf_op jit(solution)/shard_map/forward/pallas_call | solution.py:187
  69.5 556.8 %reduce_tiles.1 = (f32[27648,768]{1,0:T(8,128)}, f32[8,768]{1,0:T(8,128)}, bf16[384,768]{1,0:T(8,128)(2,1)}, bf16[3,384,2304]{2,1,0:T(8,128)(2,1)}, bf16[3,384,7...) custom-call(bf16[3,384,768]{2,1,0:T(8,128)(2,1)} %get-tuple-element.22.refs_0_, ...), custom_call_target="tpu_custom_call" | custom-call | flops 16307453952 | bytes 169869312 | tf_op jit(solution)/shard_map/reduce_tiles/pallas_call | solution.py:717
  626.2 1.4 fusion
  627.6 0.0 copy-start
  627.6 56.3 %spread_tiles.1 = (f32[3,768,2304]{2,1,0:T(8,128)}, f32[3,768,768]{2,1,0:T(8,128)}, f32[3,768,3072]{2,1,0:T(8,128)}, f32[3,3072,768]{2,1,0:T(8,128)}) custom-call(f32[27648,768]{1,0:T(8,128)} %get-tuple-element.32.src_ref), custom_call_target="tpu_custom_call" | custom-call | tf_op jit(solution)/shard_map/spread_tiles/pallas_call | solution.py:773
  684.0 0.0 copy-done
  684.0 0.8 copy.16
Async XLA Ops:
  627.6 56.3 %copy-start = (bf16[384,768]{1,0:T(8,128)(2,1)S(1)}, bf16[384,768]{1,0:T(8,128)(2,1)}, u32[]{:S(2)}) copy-start(bf16[384,768]{1,0:T(8,128)(2,1)} %get-tuple-element.30) | copy-start | bytes 1769476
